TPU v7x, 32 devices: a 4x2x2 block of a 4x4x8 slice. The times are simulated.
32 devices in a mesh: dp: 4 (over y, z), tp: 8 (over x, core).
Axes of the slice: x: 4, y: 2, z: 2, core: 2. Of those that a mesh axis runs over, the one named last changes fastest.
The devices are a block of a 4x4x8 slice.
Arguments:
- hidden: bfloat16 [48, 512, 2560], P('dp', 'tp'), parts along dimension 0
- lengths: int32 [48], P('dp'), parts along dimension 0
- rope_cos: float32 [48, 512, 16], P('dp'), parts along dimension 0
- rope_sin: float32 [48, 512, 16], P('dp'), parts along dimension 0
- cache_lat: bfloat16 [48, 1024, 256], P('dp'), parts along dimension 0
- cache_pe: bfloat16 [48, 1024, 32], P('dp'), parts along dimension 0
- norm_in: float32 [2560], replicated
- w_dq: bfloat16 [2560, 768], replicated
- norm_q: float32 [768], replicated
- w_dkv: bfloat16 [2560, 288], replicated
- norm_kv: float32 [256], replicated
- w_uq: bfloat16 [768, 40, 96], P(None, 'tp')
- w_uk: bfloat16 [256, 40, 64], P(None, 'tp')
- w_uv: bfloat16 [256, 40, 64], P(None, 'tp')
- w_out: bfloat16 [2560, 2560], P('tp')
Outputs:
- output 1: bfloat16 [48, 512, 2560], P('dp', 'tp'), parts along dimension 0
- output 2: bfloat16 [48, 1024, 256], P('dp'), parts along dimension 0
- output 3: bfloat16 [48, 1024, 32], P('dp'), parts along dimension 0
There are 4 independent parts. A program takes and returns all parts, laid end to end along the dimension named above; an argument that names none is the same for every part.
All inputs are finite; a program needn't handle non-finite values.
Results may differ from a plain program's by a relative error of at most 0.0169221.
Values are sent between devices in bfloat16 or wider.
A program may use at most 768 MiB of HBM per device.

v0:
```python
import jax
import jax.numpy as jnp
from jax import lax
from jax.sharding import PartitionSpec as P


def rms_norm(values, gain_vec):
    inv_rms = lax.rsqrt(jnp.mean(values * values, axis=-1, keepdims=True) + 1e-6)
    return values * inv_rms * gain_vec


def apply_rope(values, cos_tab, sin_tab):
    half_dim = values.shape[-1] // 2
    lower_half = values[..., :half_dim]
    upper_half = values[..., half_dim:]
    return jnp.concatenate([lower_half * cos_tab - upper_half * sin_tab, upper_half * cos_tab + lower_half * sin_tab], axis=-1)


def write_rows(old_rows, new_rows, start_row):
    return lax.dynamic_update_slice(old_rows, new_rows, (start_row, 0))


def solution(mesh):
    def local_step(hidden, lengths, rope_cos, rope_sin, cache_lat, cache_pe, norm_in, w_dq, norm_q, w_dkv, norm_kv, w_uq, w_uk, w_uv, w_out):
        gathered = lax.all_gather(hidden, "tp", axis=1, tiled=True)
        chunk_len = gathered.shape[1]
        model_dim = gathered.shape[2]
        kv_rank, heads_local, nope_dim = w_uk.shape
        value_dim = w_uv.shape[2]
        rope_dim = cache_pe.shape[2]
        cache_len = cache_lat.shape[1]
        normed = rms_norm(gathered.astype(jnp.float32), norm_in).astype(jnp.bfloat16)
        q_latent = rms_norm(jnp.einsum("btd,dq->btq", normed, w_dq, preferred_element_type=jnp.float32), norm_q).astype(jnp.bfloat16)
        kv_proj = jnp.einsum("btd,dk->btk", normed, w_dkv, preferred_element_type=jnp.float32)
        new_lat = rms_norm(kv_proj[..., :kv_rank], norm_kv).astype(jnp.bfloat16)
        new_pe = apply_rope(kv_proj[..., kv_rank:], rope_cos, rope_sin).astype(jnp.bfloat16)
        lat_all = jax.vmap(write_rows)(cache_lat, new_lat, lengths)
        pe_all = jax.vmap(write_rows)(cache_pe, new_pe, lengths)
        q_full = jnp.einsum("btq,qhd->bthd", q_latent, w_uq, preferred_element_type=jnp.float32)
        q_nope = q_full[..., :nope_dim].astype(jnp.bfloat16)
        q_pe = apply_rope(q_full[..., nope_dim:], rope_cos[:, :, None, :], rope_sin[:, :, None, :]).astype(jnp.bfloat16)
        keys_nope = jnp.einsum("bsc,chd->bshd", lat_all, w_uk, preferred_element_type=jnp.float32).astype(jnp.bfloat16)
        values_all = jnp.einsum("bsc,chv->bshv", lat_all, w_uv, preferred_element_type=jnp.float32).astype(jnp.bfloat16)
        scores = jnp.einsum("bthd,bshd->bhts", q_nope, keys_nope, preferred_element_type=jnp.float32)
        scores = scores + jnp.einsum("bthr,bsr->bhts", q_pe, pe_all, preferred_element_type=jnp.float32)
        key_pos = jnp.arange(cache_len)[None, None, :]
        row_limit = lengths[:, None, None] + jnp.arange(chunk_len)[None, :, None] + 1
        visible = (key_pos < row_limit)[:, None, :, :]
        scores = jnp.where(visible, scores * ((nope_dim + rope_dim) ** -0.5), -1e30)
        attn_probs = jax.nn.softmax(scores, axis=-1).astype(jnp.bfloat16)
        attn_out = jnp.einsum("bhts,bshv->bthv", attn_probs, values_all, preferred_element_type=jnp.float32).astype(jnp.bfloat16)
        out_heads = w_out.reshape(heads_local, value_dim, model_dim)
        head_sum = jnp.einsum("bthv,hvd->btd", attn_out, out_heads, preferred_element_type=jnp.float32)
        reduced = lax.psum_scatter(head_sum, "tp", scatter_dimension=1, tiled=True)
        return (reduced + hidden.astype(jnp.float32)).astype(jnp.bfloat16), lat_all, pe_all

    spec_tok = P("dp", "tp", None)
    spec_len = P("dp")
    spec_seq = P("dp", None, None)
    spec_vec = P(None)
    spec_mat = P(None, None)
    spec_head = P(None, "tp", None)
    spec_rows = P("tp", None)
    in_specs = (spec_tok, spec_len, spec_seq, spec_seq, spec_seq, spec_seq, spec_vec, spec_mat, spec_vec, spec_mat, spec_vec, spec_head, spec_head, spec_head, spec_rows)
    return jax.shard_map(local_step, mesh=mesh, in_specs=in_specs, out_specs=(spec_tok, spec_seq, spec_seq), check_vma=False)
```

profile of v0, /device:TPU:81, one launch (start us, length us, event | category | flops | bytes accessed | tf_op | source)
XLA Modules:
  0.0 1023.4 jit_solution(6316769844066992833)
XLA Ops:
  7.3 6.0 copy.46
  13.6 5.6 iota_compare_fusion
  19.2 143.5 %all-gather.2.cloned.1.call-done = bf16[12,512,2560]{2,1,0:T(8,128)(2,1)} async-done(((bf16[12,64,2560]{2,1,0:T(8,128)(2,1)}), bf16[12,512,2560]{2,1,0:T(8,128)(2,1)}) %all-gather.2.cloned.1.call-update) | async-done | bytes 31457296 | tf_op jit(solution)/shard_map/all_gather | solution.py:25
  162.7 11.0 %fusion.3 = f32[12,512]{1,0:T(8,128)S(1)} fusion(bf16[12,512,2560]{2,1,0:T(8,128)(2,1)} %all-gather.2.cloned.1.call-done), kind=kLoop, calls=%fused_computation.15 | loop fusion | flops 47179776 | bytes 31481856 | tf_op jit(solution)/shard_map/reduce_sum | solution.py:8
  173.7 17.4 %fusion.9 = f32[12,512,288]{1,2,0:T(8,128)} fusion(bf16[12,512,2560]{2,1,0:T(8,128)(2,1)} %all-gather.2.cloned.1.call-done, f32[2560]{0:T(1024)S(1)} %copy-done.14, f32[12,512]{1,0:T(8,128)S(1)} %add_rsqrt_fusion.2, bf16[2560,288]{0,1:T(8,128)(2,1)} %param.24), kind=kOutput, calls=%fused_computation.22 | convolution fusion | flops 9122611200 | bytes 40044544 | tf_op jit(solution)/shard_map/btd,dk->btk/dot_general | solution.py:34
  191.1 3.6 multiply_reduce_fusion.1
  194.8 5.6 multiply_convert_fusion.1
  200.4 137.3 %while.2 = (s32[]{:T(128)}, bf16[12,1024,256]{2,1,0:T(8,128)(2,1)}, s32[12,3]{0,1:T(4,128)S(1)}, bf16[12,512,256]{1,2,0:T(8,128)(2,1)}, s32[]{:T(128)}, /*index=5*/s32[3]{0:T(128)S(1)}, s32[]{:T(128)}) while((s32[]{:T(128)}, bf16[12,1024,256]{2,1,0:T(8,128)(2,1)}, s32[12,3]{0,1:T(4,128)S(1)}, bf16[12,512,256]{1,2,0:T(8,128)(2,1)}, s32[]{:T(128)}, ...), condition=%wide.while_cond, body=%wide.while_body.sunk | while | flops 131091 | bytes 2359467 | solution.py:20
  204.9 3.0 dynamic-slice_select_fusion.4
  207.9 4.1 dynamic-update-slice.6
  219.5 3.2 dynamic-update-slice.6
  230.2 4.1 dynamic-update-slice.6
  241.8 4.1 dynamic-update-slice.6
  253.4 3.9 dynamic-update-slice.6
  264.8 4.0 dynamic-update-slice.6
  276.3 4.1 dynamic-update-slice.6
  287.9 4.0 dynamic-update-slice.6
  299.3 3.9 dynamic-update-slice.6
  310.7 3.8 dynamic-update-slice.6
  322.0 4.1 dynamic-update-slice.6
  333.6 4.1 dynamic-update-slice.6
  337.7 32.7 %multiply_reduce_fusion = (f32[12,512]{1,0:T(8,128)S(1)}, f32[12,512,768]{2,1,0:T(8,128)}) fusion(bf16[2560,768]{1,0:T(8,128)(2,1)} %param.22, bf16[12,512,2560]{2,1,0:T(8,128)(2,1)} %all-gather.2.cloned.1.call-done, f32[2560]{0:T(1024)S(1)} %copy-done.14, f32[12,512]{1,0:T(8,128)S(1)} %add_rsqrt_fusion.2), kind=kOutput, calls=%fused_computation.24 | convolution fusion | flops 24231536640 | bytes 54323200 | tf_op jit(solution)/shard_map/btd,dq->btq/dot_general | solution.py:33
  372.6 90.5 %while.3 = (s32[]{:T(128)}, bf16[12,1024,32]{1,2,0:T(8,128)(2,1)S(1)}, s32[12,3]{0,1:T(4,128)S(1)}, bf16[12,512,32]{1,2,0:T(8,128)(2,1)}, s32[]{:T(128)}, /*index=5*/s32[3]{0:T(128)S(1)}, s32[]{:T(128)}) while((s32[]{:T(128)}, bf16[12,1024,32]{1,2,0:T(8,128)(2,1)S(1)}, s32[12,3]{0,1:T(4,128)S(1)}, bf16[12,512,32]{1,2,0:T(8,128)(2,1)}, s32[]{:T(128)}, ...), condition=%wide.while_cond.1, body=%wide.while_body.1.sunk | while | flops 16403 | bytes 164011 | solution.py:20
  464.0 9.3 fusion.12
  473.3 4.2 copy-done.1
  479.3 48.0 %fusion.16 = f32[12,5,512,1024]{3,2,1,0:T(8,128)} fusion(bf16[12,1024,256]{2,1,0:T(8,128)(2,1)} %get-tuple-element.8, f32[12,512,5,96]{1,3,2,0:T(8,128)} %copy-done.1, bf16[256,5,64]{0,2,1:T(8,128)(2,1)S(1)} %copy-done.2), kind=kOutput, calls=%fused_computation.31 | convolution fusion | flops 6043729920 | bytes 136216576 | tf_op jit(solution)/shard_map/bthd,bshd->bhts/dot_general | solution.py:44
  527.4 8.1 fusion.21
  535.5 95.6 %fusion.47 = (f32[12,5,512]{2,1,0:T(8,128)S(1)}, f32[12,5,512,1024]{3,2,1,0:T(8,128)}) fusion(f32[12,5,512,1024]{3,2,1,0:T(8,128)} %fusion.16, pred[12,512,1024]{2,1,0:T(8,128)(4,1)} %iota_compare_fusion, bf16[12,512,5,16]{1,3,2,0:T(8,128)(2,1)} %get-tuple-element.50, bf16[12,512,5,16]{1,3,2,0:T(8,128)(2,1)S(1)} %get-tuple-element.49, ...), kind=kOutput, calls=%fused_computation.67 | convolution fusion | flops 2174485504 | bytes 260825088 | tf_op jit(solution)/shard_map/sub | solution.py:50
  631.0 44.3 %fusion.69 = bf16[12,512,5,64]{1,3,2,0:T(8,128)(2,1)} fusion(f32[12,5,512,1024]{3,2,1,0:T(8,128)} %get-tuple-element.56, f32[12,5,512]{2,1,0:T(8,128)S(1)} %get-tuple-element.55, bf16[12,1024,5,64]{1,3,2,0:T(8,128)(2,1)} %fusion.21), kind=kOutput, calls=%fused_computation.40.clone.1 | convolution fusion | flops 4091412480 | bytes 137748480 | tf_op jit(solution)/shard_map/bhts,bshv->bthv/dot_general | solution.py:51
  675.4 26.8 %convolution_bitcast_fusion = f32[12,512,2560]{2,1,0:T(8,128)} fusion(bf16[5,64,2560,1]{2,1,0,3:T(8,128)(2,1)S(1)} %bitcast.107, bf16[12,512,5,64]{1,3,2,0:T(8,128)(2,1)} %fusion.69), kind=kOutput, calls=%fused_computation.19 | convolution fusion | flops 10066329600 | bytes 68485120 | tf_op jit(solution)/shard_map/bthv,hvd->btd/dot_general | solution.py:53
  702.3 306.8 %reduce-scatter.2.cloned.1.call-done = f32[12,64,2560]{2,1,0:T(8,128)} async-done(((f32[12,512,2560]{2,1,0:T(8,128)}), f32[12,64,2560]{2,1,0:T(8,128)}) %reduce-scatter.2.cloned.1.call-update) | async-done | bytes 7864336 | tf_op jit(solution)/shard_map/reduce_scatter | solution.py:54
  1009.1 7.5 add_convert_fusion
  (175 shorter events, 182.3 us)
Async XLA Ops:
  7.2 668.2 %copy-start = (bf16[320,2560]{1,0:T(8,128)(2,1)S(1)}, bf16[320,2560]{1,0:T(8,128)(2,1)}, u32[]{:S(2)}) copy-start(bf16[320,2560]{1,0:T(8,128)(2,1)} %param.29) | copy-start | bytes 4915204
  7.2 6.2 copy-start.13
  7.2 6.2 copy-start.12
  7.2 155.5 %all-gather.2.cloned.1.call-start = ((), (), s32[]{:S(2)}) async-start(), calls=%async_computation.1 | async-start | bytes 35389440 | tf_op jit(solution)/shard_map/all_gather | solution.py:25
  13.3 995.7 %reduce-scatter.2.cloned.1.call-start = ((), (), s32[]{:S(2)}) async-start(), calls=%async_computation.2 | async-start | bytes 70778880 | tf_op jit(solution)/shard_map/reduce_scatter | solution.py:54
  19.2 154.5 %copy-start.14 = (f32[2560]{0:T(1024)S(1)}, f32[2560]{0:T(1024)}, u32[]{:S(2)}) copy-start(f32[2560]{0:T(1024)} %param.21) | copy-start | bytes 30724
  173.7 21.1 %copy-start.11 = (f32[256]{0:T(256)S(1)}, f32[256]{0:T(256)}, u32[]{:S(2)}) copy-start(f32[256]{0:T(256)} %param.25) | copy-start | bytes 3076
  191.1 9.3 copy-start.9
  337.7 32.8 %copy-start.5 = (f32[12,512,16]{1,2,0:T(8,128)S(1)}, f32[12,512,16]{1,2,0:T(8,128)}, u32[]{:S(2)}) copy-start(f32[12,512,16]{1,2,0:T(8,128)} %param.18) | copy-start | bytes 1179652
  337.7 32.8 %copy-start.6 = (f32[12,512,16]{1,2,0:T(8,128)S(1)}, f32[12,512,16]{1,2,0:T(8,128)}, u32[]{:S(2)}) copy-start(f32[12,512,16]{1,2,0:T(8,128)} %param.17) | copy-start | bytes 1179652
  337.7 34.9 %copy-start.4 = (bf16[12,1024,32]{1,2,0:T(8,128)(2,1)S(1)}, bf16[12,1024,32]{1,2,0:T(8,128)(2,1)}, u32[]{:S(2)}) copy-start(bf16[12,1024,32]{1,2,0:T(8,128)(2,1)} %param.20) | copy-start | bytes 2359300
  337.7 126.3 %copy-start.10 = (f32[768]{0:T(1024)S(1)}, f32[768]{0:T(1024)}, u32[]{:S(2)}) copy-start(f32[768]{0:T(1024)} %param.23) | copy-start | bytes 9220
  463.1 0.9 copy-start.3
  464.0 13.5 %copy-start.7 = (f32[12,512,16]{1,2,0:T(8,128)S(1)}, f32[12,512,16]{1,2,0:T(8,128)}, u32[]{:S(2)}) copy-start(f32[12,512,16]{1,2,0:T(8,128)} %param.17) | copy-start | bytes 1179652
  473.3 4.2 copy-start.1
  477.6 1.8 copy-start.2
  479.3 48.0 %copy-start.8 = (bf16[256,5,64]{0,2,1:T(8,128)(2,1)S(1)}, bf16[256,5,64]{0,2,1:T(8,128)(2,1)}, u32[]{:S(2)}) copy-start(bf16[256,5,64]{0,2,1:T(8,128)(2,1)} %param.28) | copy-start | bytes 491524
Sparse Core Ops, SparseCore 0:
  13.5 149.1 all-gather.1
  702.4 306.6 reduce-scatter.1
where the time goes:
time: 1030 us; the launch traced here: 1020 us
  waiting for transfers between devices  450 us (44%)
  matrix products  282 us (27%)
  other arithmetic  168 us (16%)
  local copies, waits for them, and re-layouts  108 us (10%)
  between operations  14.2 us (1%)
    reduce_scatter x1, waiting for transfers between devices, local_step(): reduced = lax.psum_scatter(head_sum, 'tp', scatter_dimension=1, tiled=True)  307 us
    all_gather x1, waiting for transfers between devices, local_step(): gathered = lax.all_gather(hidden, 'tp', axis=1, tiled=True)  143 us
    scatter x48, other arithmetic  131 us
    scatter x96, local copies, waits for them, and re-layouts  96.4 us
    sub x1, matrix products, local_step(): attn_probs = jax.nn.softmax(scores, axis=-1).astype(jnp.bfloat16)  95.6 us
    dot_general x1, matrix products, local_step(): jnp.einsum('bthd,bshd->bhts', q_nope, keys_nope, preferred_element_type=j...  48 us
    dot_general x1, matrix products, local_step(): jnp.einsum('bhts,bshv->bthv', attn_probs, values_all, preferred_element_t...  44.3 us
    dot_general x1, matrix products, local_step(): jnp.einsum('btd,dq->btq', normed, w_dq, preferred_element_type=jnp.float32)  32.7 us
  transfers between devices with their start and end apart: 2, of which 2 were waited for; matrix products, arithmetic and copies ran while one was open for 1% of the time, Pallas kernels for 0%

commit v1 on v0

v1 whole, which is shorter than its diff:
```python
import functools

import jax
import jax.numpy as jnp
from jax import lax
from jax.experimental import pallas as pl
from jax.experimental.pallas import tpu as pltpu
from jax.sharding import PartitionSpec as P

BLOCK = 128
LOG2E = 1.4426950408889634
F32 = jnp.float32
BF16 = jnp.bfloat16


def dot(a, b):
    return lax.dot_general(a, b, (((1,), (0,)), ((), ())), preferred_element_type=F32)


def dot_t(a, b):
    return lax.dot_general(a, b, (((1,), (1,)), ((), ())), preferred_element_type=F32)


def project_kernel(where_ref, x_ref, g1_ref, wdq_ref, gq_ref, wkv_ref, gkv_ref, cos_ref, sin_ref, cq_ref, kv_ref):
    seqs, toks, dim = x_ref.shape
    rank = gkv_ref.shape[1]
    half = cos_ref.shape[1]
    odd = where_ref[1]
    x = x_ref[...].reshape(seqs * toks, dim).astype(F32)
    inv = lax.rsqrt(jnp.mean(x * x, axis=-1, keepdims=True) + 1e-6)
    a = (x * inv * g1_ref[...]).astype(BF16)
    kv = dot_t(a, wkv_ref[...])
    c = kv[:, :rank]
    inv = lax.rsqrt(jnp.mean(c * c, axis=-1, keepdims=True) + 1e-6)
    kv_ref[:, :, :rank] = (c * inv * gkv_ref[...]).astype(BF16).reshape(seqs, toks, rank)
    for s in range(seqs):
        cos_pair, sin_pair = cos_ref[s], sin_ref[s]
        cos = jnp.where(odd == 1, cos_pair[:, toks:], cos_pair[:, :toks])
        sin = jnp.where(odd == 1, sin_pair[:, toks:], sin_pair[:, :toks])
        table = jnp.concatenate([cos, cos, -sin, sin], axis=0).T
        p = kv[s * toks : (s + 1) * toks, rank:]
        swapped = jnp.concatenate([p[:, half:], p[:, :half]], axis=1)
        kv_ref[s, :, rank:] = (p * table[:, : 2 * half] + swapped * table[:, 2 * half :]).astype(BF16)
    h = dot(a, wdq_ref[...])
    inv = lax.rsqrt(jnp.mean(h * h, axis=-1, keepdims=True) + 1e-6)
    cq_ref[...] = (h * inv * gq_ref[...]).astype(BF16).reshape(cq_ref.shape)


def attend_kernel(
    where_ref,
    len_ref,
    wq_ref,
    wkv_ref,
    cq_ref,
    cos_ref,
    sin_ref,
    new_ref,
    lat_ref,
    pe_ref,
    own_ref,
    send_ref,
    lat_out,
    pe_out,
    qraw,
    qbd,
    rows,
    rot,
    kbuf,
    vbuf,
    s_a,
    s_b,
    pbuf,
    obuf,
    fresh,
    fresh_pe,
):
    step = pl.program_id(0)
    chip, odd = where_ref[0], where_ref[1]
    peers, seqs, toks, _ = new_ref.shape
    rank = lat_ref.shape[2]
    rope = pe_ref.shape[1]
    half = rope // 2
    shards, q_rows, q_rank = wq_ref.shape
    kv_rows = wkv_ref.shape[1] // 2
    nope = qbd.shape[2] // 4
    head = nope + rope
    local_heads = q_rows // head
    pairs = qbd.shape[1]
    cache_len = lat_ref.shape[1]
    chunk = peers * toks
    width = 2 * BLOCK
    factor = LOG2E * head**-0.5

    @pl.when(step == 0)
    def _():
        qbd[...] = jnp.zeros_like(qbd)
        rot[...] = jnp.zeros_like(rot)
        fresh_pe[...] = jnp.zeros_like(fresh_pe)

    cq = jnp.concatenate([cq_ref[c, s] for s in range(seqs) for c in range(2)], axis=0)
    for shard in range(shards):
        qraw[...] = dot_t(wq_ref[shard], cq)
        for h in range(local_heads):
            index = shard * local_heads + h
            pair, side = index // 2, index % 2
            base = h * head
            for s in range(seqs):
                lanes = slice(s * BLOCK, (s + 1) * BLOCK)
                cols = slice(side * BLOCK, (side + 1) * BLOCK)
                qbd[s, pair, side * nope : (side + 1) * nope, cols] = qraw[base : base + nope, lanes].astype(BF16)
                lo = qraw[base + nope : base + nope + half, lanes]
                hi = qraw[base + nope + half : base + head, lanes]
                cos, sin = cos_ref[s], sin_ref[s]
                qbd[s, pair, 2 * nope : 2 * nope + half, cols] = (lo * cos - hi * sin).astype(BF16)
                qbd[s, pair, 2 * nope + half : 2 * nope + rope, cols] = (hi * cos + lo * sin).astype(BF16)

    def one_sequence(s, _):
        length = len_ref[step * seqs + s]
        prefix_blocks = (length + BLOCK - 1) // BLOCK
        last = prefix_blocks - 1
        total = prefix_blocks + chip + 1
        old_pe = pe_ref[s].astype(F32)

        def new_block(b, at):
            for c in range(2):
                piece = new_ref[2 * b + c, s]
                start = pl.multiple_of(at + c * toks, toks)
                rows[pl.ds(start, toks), :] = piece[:, :rank]
                rot[pl.ds(start, toks), :rope] = piece[:, rank:]

        def old_block(b, at):
            start = pl.multiple_of(b * BLOCK, BLOCK)
            rows[pl.ds(at, BLOCK), :] = lat_ref[s, pl.ds(start, BLOCK), :]
            rot[pl.ds(at, BLOCK), :rope] = pe_ref[s, :, pl.ds(start, BLOCK)].astype(F32).T.astype(BF16)

        new_block(chip, 0)
        old_block(last, BLOCK)

        def place_old(b, _):
            old_block(b, pl.multiple_of((2 + b) * BLOCK, BLOCK))
            return 0

        def place_new(b, _):
            new_block(b, pl.multiple_of((2 + last + b) * BLOCK, BLOCK))
            return 0

        lax.fori_loop(0, last, place_old, 0)
        lax.fori_loop(0, chip, place_new, 0)

        def attend(blocks):
            t = blocks * BLOCK
            for j in range(shards * kv_rows // width):
                lo = j * width
                parts = []
                while lo < (j + 1) * width:
                    shard, at = lo // kv_rows, lo % kv_rows
                    take = min(kv_rows - at, (j + 1) * width - lo)
                    parts.append((shard, at, take))
                    lo += take
                wk = jnp.concatenate([wkv_ref[g, at : at + n] for g, at, n in parts], axis=0)
                wv = jnp.concatenate([wkv_ref[g, kv_rows + at : kv_rows + at + n] for g, at, n in parts], axis=0)
                k = dot_t(rows[:t], wk).astype(BF16)
                kbuf[2 * j, :t] = k[:, :BLOCK]
                kbuf[2 * j + 1, :t] = k[:, BLOCK:]
                vbuf[2 * j : 2 * j + 2, :, :t] = dot_t(wv, rows[:t]).astype(BF16).reshape(2, BLOCK, t)

            lane = lax.broadcasted_iota(jnp.int32, (BLOCK, width), 1) % BLOCK
            row = lax.broadcasted_iota(jnp.int32, (BLOCK, width), 0)
            near = row <= lane
            tail = row < length - last * BLOCK

            def score(pair, out):
                keys = jnp.concatenate([kbuf[pair, :t], rot[:t]], axis=1)
                value = dot(keys, qbd[s, pair])
                top = jnp.where(near, value[:BLOCK], -1e30)
                out[:BLOCK] = top
                second = jnp.where(tail, value[BLOCK : 2 * BLOCK], -1e30)
                out[BLOCK : 2 * BLOCK] = second
                most = jnp.maximum(top, second)
                for b in range(2, blocks):
                    part = value[b * BLOCK : (b + 1) * BLOCK]
                    out[b * BLOCK : (b + 1) * BLOCK] = part
                    most = jnp.maximum(most, part)
                return jnp.max(most, axis=0, keepdims=True)

            def mix(pair, source, most):
                total = jnp.zeros((8, width), F32)
                for b in range(blocks):
                    e = jnp.exp2((source[b * BLOCK : (b + 1) * BLOCK] - most) * factor)
                    total = total + jnp.sum(e.reshape(BLOCK // 8, 8, width), axis=0)
                    pbuf[b * BLOCK : (b + 1) * BLOCK] = e.astype(BF16)
                inv = 1.0 / jnp.sum(total, axis=0, keepdims=True)
                o = dot(vbuf[pair, :, :t], pbuf[:t]) * inv
                obuf[pair, :nope] = o[:nope, :BLOCK].astype(BF16)
                obuf[pair, nope:] = o[nope:, BLOCK:].astype(BF16)

            def two_pairs(j, most):
                most_b = score(2 * j + 1, s_b)
                mix(2 * j, s_a, most)
                most = score(jnp.minimum(2 * j + 2, pairs - 1), s_a)
                mix(2 * j + 1, s_b, most_b)
                return most

            lax.fori_loop(0, pairs // 2, two_pairs, score(0, s_a))

        for blocks in range(2, cache_len // BLOCK + 1):
            pl.when(total == blocks)(functools.partial(attend, blocks))

        for pair in range(pairs):
            o = obuf[pair].astype(F32).T.astype(BF16)
            cols = slice(pair * BLOCK, (pair + 1) * BLOCK)
            first, second = o[:toks], o[toks:]
            own_ref[s, :, cols] = jnp.where(odd == 1, second, first)
            send_ref[s, :, cols] = jnp.where(odd == 1, first, second)

        lat_out[s] = lat_ref[s]
        for c in range(peers):
            piece = new_ref[c, s].astype(F32)
            for w in range(rank // BLOCK):
                fresh[w, BLOCK + c * toks : BLOCK + (c + 1) * toks] = piece[:, w * BLOCK : (w + 1) * BLOCK]
        base = (length // 16) * 16
        skew = length - base
        tile_row = lax.broadcasted_iota(jnp.int32, (16, BLOCK), 0)

        def shift(k, _):
            at = pl.multiple_of(base + k * 16, 16)
            for w in range(rank // BLOCK):
                moved = fresh[w, pl.ds(BLOCK - skew + k * 16, 16), :]
                local = tile_row + k * 16 - skew
                cols = slice(w * BLOCK, (w + 1) * BLOCK)
                old = lat_ref[s, pl.ds(at, 16), cols].astype(F32)
                lat_out[s, pl.ds(at, 16), cols] = jnp.where((local >= 0) & (local < chunk), moved, old).astype(BF16)
            return 0

        lax.fori_loop(0, chunk // 16 + (skew > 0).astype(jnp.int32), shift, 0)
        for b in range(cache_len // BLOCK):
            fresh_pe[b * BLOCK : (b + 1) * BLOCK, :rope] = old_pe[:, b * BLOCK : (b + 1) * BLOCK].T
        for c in range(peers):
            fresh_pe[pl.ds(length + c * toks, toks), :rope] = new_ref[c, s, :, rank:].astype(F32)
        for b in range(cache_len // BLOCK):
            pe_out[s, :, b * BLOCK : (b + 1) * BLOCK] = fresh_pe[b * BLOCK : (b + 1) * BLOCK].T[:rope].astype(BF16)
        return 0

    lax.fori_loop(0, seqs, one_sequence, 0)


def output_kernel(where_ref, own_ref, other_ref, w_ref, x_ref, y_ref):
    odd = where_ref[1]
    seqs, toks, depth = own_ref.shape
    shards = w_ref.shape[0] // 2

    def side(o, parity):
        w = jnp.concatenate([w_ref[2 * g + parity] for g in range(shards)], axis=0)
        return dot(o[...].reshape(seqs * toks, depth), w)

    y = side(own_ref, odd) + side(other_ref, 1 - odd)
    y = y + x_ref[...].reshape(y.shape).astype(F32)
    y_ref[...] = y.astype(BF16).reshape(y_ref.shape)


def solution(mesh):
    size = mesh.shape["tp"]
    even_odd = [[2 * c + p for c in range(size // 2)] for p in range(2)]
    chip_pairs = [[2 * c, 2 * c + 1] for c in range(size // 2)]
    swap = [(i, i ^ 1) for i in range(size)]

    def local_step(hidden, lengths, rope_cos, rope_sin, cache_lat, cache_pe, norm_in, w_dq, norm_q, w_dkv, norm_kv, w_uq, w_uk, w_uv, w_out):
        seqs, toks, dim = hidden.shape
        q_rank = w_dq.shape[1]
        rank, heads, nope = w_uk.shape
        rope = cache_pe.shape[2]
        cache_len = cache_lat.shape[1]
        chips = size // 2
        head = nope + rope
        pairs = chips * heads // 2
        index = lax.axis_index("tp")
        where = jnp.stack([index // 2, index % 2]).astype(jnp.int32)

        wq = w_uq.transpose(1, 2, 0).reshape(heads * head, q_rank)
        wkv = jnp.concatenate([w.transpose(1, 2, 0).reshape(heads * nope, rank) for w in (w_uk, w_uv)], axis=0)
        wkv_all = lax.all_gather(wkv, "tp", axis_index_groups=even_odd)
        wq_all = lax.all_gather(wq, "tp", axis_index_groups=even_odd)
        cos_t, sin_t = rope_cos.transpose(0, 2, 1), rope_sin.transpose(0, 2, 1)
        pe_t = cache_pe.transpose(0, 2, 1)
        wkv_down = w_dkv.transpose(1, 0)

        group = 4
        whole = lambda shape: pl.BlockSpec(shape, lambda i, w: (0,) * len(shape), pipeline_mode=pl.Buffered(1))
        cq, kv = pl.pallas_call(
            project_kernel,
            grid_spec=pltpu.PrefetchScalarGridSpec(
                num_scalar_prefetch=1,
                grid=(seqs // group,),
                in_specs=[
                    pl.BlockSpec((group, toks, dim), lambda i, w: (i, 0, 0)),
                    whole((1, dim)),
                    whole(w_dq.shape),
                    whole((1, q_rank)),
                    whole(wkv_down.shape),
                    whole((1, rank)),
                    pl.BlockSpec((group, rope // 2, BLOCK), lambda i, w: (i, 0, w[0])),
                    pl.BlockSpec((group, rope // 2, BLOCK), lambda i, w: (i, 0, w[0])),
                ],
                out_specs=[
                    pl.BlockSpec((group, toks, q_rank), lambda i, w: (i, 0, 0)),
                    pl.BlockSpec((group, toks, rank + rope), lambda i, w: (i, 0, 0)),
                ],
            ),
            out_shape=[jax.ShapeDtypeStruct((seqs, toks, q_rank), BF16), jax.ShapeDtypeStruct((seqs, toks, rank + rope), BF16)],
            cost_estimate=pl.CostEstimate(flops=2 * seqs * toks * dim * (q_rank + rank + rope), bytes_accessed=12 * 2**20, transcendentals=0),
            name="project",
        )(where, hidden, norm_in[None], w_dq, norm_q[None], wkv_down, norm_kv[None], cos_t, sin_t)

        new_all = lax.all_gather(kv, "tp")
        cq_all = lax.all_gather(cq, "tp", axis_index_groups=chip_pairs)
        w_all = lax.all_gather(w_out, "tp")

        step = 2
        whole = lambda shape: pl.BlockSpec(shape, lambda i, w, n: (0,) * len(shape), pipeline_mode=pl.Buffered(1))
        o_shape = jax.ShapeDtypeStruct((seqs, toks, pairs * 2 * nope), BF16)
        own, send, lat_new, pe_new = pl.pallas_call(
            attend_kernel,
            grid_spec=pltpu.PrefetchScalarGridSpec(
                num_scalar_prefetch=2,
                grid=(seqs // step,),
                in_specs=[
                    whole(wq_all.shape),
                    whole(wkv_all.shape),
                    pl.BlockSpec((2, step, toks, q_rank), lambda i, w, n: (0, i, 0, 0)),
                    pl.BlockSpec((step, rope // 2, BLOCK), lambda i, w, n: (i, 0, w[0])),
                    pl.BlockSpec((step, rope // 2, BLOCK), lambda i, w, n: (i, 0, w[0])),
                    pl.BlockSpec((size, step, toks, rank + rope), lambda i, w, n: (0, i, 0, 0)),
                    pl.BlockSpec((step, cache_len, rank), lambda i, w, n: (i, 0, 0)),
                    pl.BlockSpec((step, rope, cache_len), lambda i, w, n: (i, 0, 0)),
                ],
                out_specs=[
                    pl.BlockSpec((step, toks, pairs * 2 * nope), lambda i, w, n: (i, 0, 0)),
                    pl.BlockSpec((step, toks, pairs * 2 * nope), lambda i, w, n: (i, 0, 0)),
                    pl.BlockSpec((step, cache_len, rank), lambda i, w, n: (i, 0, 0)),
                    pl.BlockSpec((step, rope, cache_len), lambda i, w, n: (i, 0, 0)),
                ],
                scratch_shapes=[
                    pltpu.VMEM((heads * head, step * BLOCK), F32),
                    pltpu.VMEM((step, pairs, 2 * BLOCK, 2 * BLOCK), BF16),
                    pltpu.VMEM((cache_len, rank), BF16),
                    pltpu.VMEM((cache_len, BLOCK), BF16),
                    pltpu.VMEM((pairs, cache_len, BLOCK), BF16),
                    pltpu.VMEM((pairs, BLOCK, cache_len), BF16),
                    pltpu.VMEM((cache_len, 2 * BLOCK), F32),
                    pltpu.VMEM((cache_len, 2 * BLOCK), F32),
                    pltpu.VMEM((cache_len, 2 * BLOCK), BF16),
                    pltpu.VMEM((pairs, BLOCK, BLOCK), BF16),
                    pltpu.VMEM((rank // BLOCK, size * toks + 2 * BLOCK, BLOCK), F32),
                    pltpu.VMEM((cache_len, BLOCK), F32),
                ],
            ),
            out_shape=[
                o_shape,
                o_shape,
                jax.ShapeDtypeStruct(cache_lat.shape, BF16),
                jax.ShapeDtypeStruct(pe_t.shape, BF16),
            ],
            compiler_params=pltpu.CompilerParams(vmem_limit_bytes=60 * 2**20),
            cost_estimate=pl.CostEstimate(flops=40 * 10**9, bytes_accessed=30 * 2**20, transcendentals=30 * 10**6),
            name="attend",
        )(where, lengths, wq_all, wkv_all, cq_all, cos_t, sin_t, new_all, cache_lat, pe_t)

        other = lax.ppermute(send, "tp", swap)

        wide = 512
        y = pl.pallas_call(
            output_kernel,
            grid_spec=pltpu.PrefetchScalarGridSpec(
                num_scalar_prefetch=1,
                grid=(dim // wide,),
                in_specs=[
                    pl.BlockSpec(own.shape, lambda i, w: (0, 0, 0), pipeline_mode=pl.Buffered(1)),
                    pl.BlockSpec(own.shape, lambda i, w: (0, 0, 0), pipeline_mode=pl.Buffered(1)),
                    pl.BlockSpec(w_all.shape[:2] + (wide,), lambda i, w: (0, 0, i)),
                    pl.BlockSpec((seqs, toks, wide), lambda i, w: (0, 0, i)),
                ],
                out_specs=pl.BlockSpec((seqs, toks, wide), lambda i, w: (0, 0, i)),
            ),
            out_shape=jax.ShapeDtypeStruct(hidden.shape, BF16),
            cost_estimate=pl.CostEstimate(flops=2 * seqs * toks * dim * dim, bytes_accessed=30 * 2**20, transcendentals=0),
            name="output",
        )(where, own, other, w_all, hidden)
        return y, lat_new, pe_new.transpose(0, 2, 1)

    spec_tok = P("dp", "tp", None)
    spec_len = P("dp")
    spec_seq = P("dp", None, None)
    spec_vec = P(None)
    spec_mat = P(None, None)
    spec_head = P(None, "tp", None)
    spec_rows = P("tp", None)
    in_specs = (spec_tok, spec_len, spec_seq, spec_seq, spec_seq, spec_seq, spec_vec, spec_mat, spec_vec, spec_mat, spec_vec, spec_head, spec_head, spec_head, spec_rows)
    return jax.shard_map(local_step, mesh=mesh, in_specs=in_specs, out_specs=(spec_tok, spec_seq, spec_seq), check_vma=False)
```

time: 1030 us -> 238 us (0.23)
  the two profiles are of different devices: /device:TPU:81 before, /device:TPU:87 now
where the time goes in v1:
time: 238 us; the launch traced here: 235 us
  Pallas kernels  117 us (49%)
  waiting for transfers between devices  96.9 us (41%)
  between operations  13.8 us (6%)
  local copies, waits for them, and re-layouts  3.85 us (2%)
  other arithmetic  2.39 us (1%)
    pallas_call x1, Pallas kernels, local_step(): pl.pallas_call(attend_kernel, grid_spec=pltpu.PrefetchScalarGridSpec(num_...  90.1 us
    all_gather x1, waiting for transfers between devices, local_step(): wq_all = lax.all_gather(wq, 'tp', axis_index_groups=even_odd)  34.9 us
    all_gather x1, waiting for transfers between devices, local_step(): new_all = lax.all_gather(kv, 'tp')  33.6 us
    all_gather x1, waiting for transfers between devices, local_step(): cq_all = lax.all_gather(cq, 'tp', axis_index_groups=chip_pairs)  15.9 us
    pallas_call x1, Pallas kernels, local_step(): pl.pallas_call(output_kernel, grid_spec=pltpu.PrefetchScalarGridSpec(num_...  15.8 us
    pallas_call x1, Pallas kernels, local_step(): pl.pallas_call(project_kernel, grid_spec=pltpu.PrefetchScalarGridSpec(num...  11.5 us
    all_gather x1, waiting for transfers between devices, local_step(): wkv_all = lax.all_gather(wkv, 'tp', axis_index_groups=even_odd)  6.83 us
  transfers between devices with their start and end apart: 6, of which 5 were waited for; matrix products, arithmetic and copies ran while one was open for 1% of the time, Pallas kernels for 43%

profile of v1, /device:TPU:87, one launch (start us, length us, event | category | flops | bytes accessed | tf_op | source)
XLA Modules:
  0.0 235.0 jit_solution(10811207899530143535)
XLA Ops:
  7.2 0.1 all-gather.12.cloned.1.call-start
  7.2 1.7 pad_maximum_fusion
  9.0 0.1 all-gather.12.cloned.1.call-update
  9.0 0.1 all-gather.14.cloned.1.call-start
  9.1 1.3 broadcast_in_dim.9.g1_ref
  10.4 1.3 broadcast_in_dim.10.gq_ref
  11.7 0.6 pad_add_fusion.where_ref
  12.4 11.5 %project.1 = (bf16[12,64,768]{2,1,0:T(8,128)(2,1)}, bf16[12,64,288]{2,1,0:T(8,128)(2,1)}) custom-call(s32[2]{0:T(128)} %pad_add_fusion.where_ref, bf16[12,64,2560]{2,1,0:T(8,128)(2,1)} %x_ref.3, f32[1,2560]{1,0:T(1,128)} %broadcast_in_dim.9.g1_ref, bf16[2560,768]{1,0:T(8,128)(2,1)} %wdq_ref.1, f32[1,768]{1,0:T(1,128)} %broadcast_in_dim.10.gq_ref, ...), custom_call_target="tpu_custom_call" | custom-call | flops 4152360960 | bytes 12582912 | tf_op jit(solution)/shard_map/project/pallas_call | solution.py:289
  23.8 0.1 all-gather.14.cloned.1.call-update
  23.9 0.1 all-gather.10.cloned.1.call-start
  24.0 0.7 all-gather.10.cloned.1.call-update
  24.7 0.1 all-gather.16.cloned.1.call-start
  24.8 0.6 all-gather.16.cloned.1.call-update
  25.3 0.1 all-gather.18.cloned.1.call-start
  25.4 0.6 all-gather.18.cloned.1.call-update
  26.0 6.8 %all-gather.12.cloned.1.call-done = bf16[2560,256]{1,0:T(8,128)(2,1)} async-done(((bf16[640,256]{1,0:T(8,128)(2,1)}), bf16[2560,256]{1,0:T(8,128)(2,1)}) %all-gather.12.cloned.1.call-update) | async-done | bytes 1310736 | tf_op jit(solution)/shard_map/all_gather | solution.py:281
  32.8 15.9 %all-gather.14.cloned.1.call-done = bf16[24,64,768]{2,1,0:T(8,128)(2,1)} async-done(((bf16[12,64,768]{2,1,0:T(8,128)(2,1)}), bf16[24,64,768]{2,1,0:T(8,128)(2,1)}) %all-gather.14.cloned.1.call-update) | async-done | bytes 2359312 | tf_op jit(solution)/shard_map/all_gather | solution.py:315
  48.7 34.9 %all-gather.10.cloned.1.call-done.wq_ref = bf16[4,480,768]{2,1,0:T(8,128)(2,1)} async-done(((bf16[1,480,768]{2,1,0:T(8,128)(2,1)}), bf16[4,480,768]{2,1,0:T(8,128)(2,1)}) %all-gather.10.cloned.1.call-update) | async-done | bytes 2949136 | tf_op jit(solution)/shard_map/all_gather | solution.py:282
  83.6 33.6 %all-gather.16.cloned.1.call-done = bf16[96,64,288]{2,1,0:T(8,128)(2,1)} async-done(((bf16[12,64,288]{2,1,0:T(8,128)(2,1)}), bf16[96,64,288]{2,1,0:T(8,128)(2,1)}) %all-gather.16.cloned.1.call-update) | async-done | bytes 3538960 | tf_op jit(solution)/shard_map/all_gather | solution.py:314
  117.2 90.1 %attend.1 = (bf16[12,64,1280]{2,1,0:T(8,128)(2,1)}, bf16[12,64,1280]{2,1,0:T(8,128)(2,1)}, bf16[12,1024,256]{2,1,0:T(8,128)(2,1)}, bf16[12,32,1024]{2,1,0:T(8,128)(2,1)}) custom-call(s32[2]{0:T(128)} %pad_add_fusion.where_ref, s32[12]{0:T(128)} %len_ref.1, bf16[4,480,768]{2,1,0:T(8,128)(2,1)} %all-gather.10.cloned.1.call-done.wq_ref, ...), custom_call_target="tpu_custom_call" | custom-call | flops 40000000000 | bytes 31457280 | tf_op jit(solution)/shard_map/attend/pallas_call | solution.py:321
  207.3 0.3 collective-permute-start
  207.7 3.7 %collective-permute-done.other_ref = bf16[12,64,1280]{2,1,0:T(8,128)(2,1)S(1)} collective-permute-done((bf16[12,64,1280]{2,1,0:T(8,128)(2,1)}, bf16[12,64,1280]{2,1,0:T(8,128)(2,1)S(1)}, u32[]{:S(2)}, u32[]{:S(2)}) %collective-permute-start) | collective-permute-done | bytes 1966112 | tf_op jit(solution)/shard_map/ppermute | solution.py:368
  211.4 0.0 copy-start
  211.4 0.0 all-gather.18.cloned.1.call-done
  211.4 1.3 copy-done
  212.6 15.8 %output.1 = bf16[12,64,2560]{2,1,0:T(8,128)(2,1)} custom-call(s32[2]{0:T(128)} %pad_add_fusion.where_ref, bf16[12,64,1280]{2,1,0:T(8,128)(2,1)} %get-tuple-element.11.own_ref, bf16[12,64,1280]{2,1,0:T(8,128)(2,1)} %copy-done, bf16[8,320,2560]{2,1,0:T(8,128)(2,1)} %bitcast.24, bf16[12,64,2560]{2,1,0:T(8,128)(2,1)} %x_ref.3), custom_call_target="tpu_custom_call" | custom-call | flops 10066329600 | bytes 31457280 | tf_op jit(solution)/shard_map/output/pallas_call | solution.py:371
Async XLA Ops:
  7.2 25.6 %all-gather.12.cloned.1.call-start = ((), (), s32[]{:S(2)}) async-start(), calls=%async_computation.1 | async-start | bytes 1638400 | tf_op jit(solution)/shard_map/all_gather | solution.py:281
  9.0 39.7 %all-gather.14.cloned.1.call-start = ((), (), s32[]{:S(2)}) async-start(), calls=%async_computation.2 | async-start | bytes 3538944 | tf_op jit(solution)/shard_map/all_gather | solution.py:315
  23.9 59.7 %all-gather.10.cloned.1.call-start = ((), (), s32[]{:S(2)}) async-start(), calls=%async_computation | async-start | bytes 3686400 | tf_op jit(solution)/shard_map/all_gather | solution.py:282
  24.7 92.5 %all-gather.16.cloned.1.call-start = ((), (), s32[]{:S(2)}) async-start(), calls=%async_computation.3 | async-start | bytes 5308416 | tf_op jit(solution)/shard_map/all_gather | solution.py:314
  25.3 186.1 %all-gather.18.cloned.1.call-start = ((), (), s32[]{:S(2)}) async-start(), calls=%async_computation.4 | async-start | bytes 14745600 | tf_op jit(solution)/shard_map/all_gather | solution.py:316
  207.3 4.1 %collective-permute-start = (bf16[12,64,1280]{2,1,0:T(8,128)(2,1)}, bf16[12,64,1280]{2,1,0:T(8,128)(2,1)S(1)}, u32[]{:S(2)}, u32[]{:S(2)}) collective-permute-start(bf16[12,64,1280]{2,1,0:T(8,128)(2,1)} %get-tuple-element.12), channel_id=1, source_target_pairs={{0,1},{1,0},{2,3},{3,2},{4,5},{5,4},{6,7},{7,6},{8,9},{9,8},{10,11... | collective-permute-start | bytes 5898248 | tf_op jit(solution)/shard_map/ppermute | solution.py:368
  211.4 1.3 copy-start
Sparse Core Ops, SparseCore 0:
  10.2 22.6 all-gather.11
  34.9 13.7 all-gather.13
  50.3 33.2 all-gather.9
  85.6 31.5 all-gather.15
  118.6 66.7 all-gather.17

commit v2 on v0

v2 whole, which is shorter than its diff:
```python
import functools

import jax
import jax.numpy as jnp
from jax import lax
from jax.experimental import pallas as pl
from jax.experimental.pallas import tpu as pltpu
from jax.sharding import PartitionSpec as P

BLOCK = 128
LOG2E = 1.4426950408889634
NEVER = -1e30
F32 = jnp.float32
BF16 = jnp.bfloat16
MESH = pl.DeviceIdType.MESH
MIB = 2**20


def dot(a, b):
    return lax.dot_general(a, b, (((1,), (0,)), ((), ())), preferred_element_type=F32)


def dot_t(a, b):
    return lax.dot_general(a, b, (((1,), (1,)), ((), ())), preferred_element_type=F32)


def unit(x):
    return x * lax.rsqrt(jnp.mean(x * x, axis=-1, keepdims=True) + 1e-6)


def project_kernel(
    size,
    x_hbm,
    g1_ref,
    wdq_hbm,
    gq_ref,
    wkv_hbm,
    gkv_ref,
    cos_ref,
    sin_ref,
    c_all,
    p_all,
    cq_pair,
    x_buf,
    wdq,
    wkv,
    a_buf,
    c_own,
    p_own,
    cq_own,
    load_sem,
    keep_sem,
    send_sem,
    recv_sem,
):
    me = lax.axis_index("tp")
    odd = lax.rem(me, 2)
    chip = me // 2
    right, left = lax.rem(me + 2, size), lax.rem(me + size - 2, size)
    other = me + 1 - 2 * odd
    seqs, toks, dim = x_hbm.shape
    groups = p_own.shape[0]
    per = seqs // groups
    rank = c_own.shape[2]
    rope = BLOCK // per
    half = rope // 2

    loads = [pltpu.make_async_copy(x_hbm.at[pl.ds(0, per)], x_buf.at[pl.ds(0, per)], load_sem.at[0])]
    loads.append(pltpu.make_async_copy(wkv_hbm, wkv, load_sem.at[1]))
    for g in range(1, groups):
        rows = pl.ds(g * per, per)
        loads.append(pltpu.make_async_copy(x_hbm.at[rows], x_buf.at[rows], load_sem.at[1 + g]))
    loads.append(pltpu.make_async_copy(wdq_hbm, wdq, load_sem.at[1 + groups]))
    for load in loads:
        load.start()

    barrier = pltpu.get_barrier_semaphore()
    for peer in (left, right, other):
        pl.semaphore_signal(barrier, inc=1, device_id={"tp": peer}, device_id_type=MESH)
    pl.semaphore_wait(barrier, 3)

    def copies(g, slot_from, slot_to, kind, peer, fresh=False):
        rows = pl.ds(g * per, per)
        c_src = c_own.at[rows] if fresh else c_all.at[rows, slot_from, odd]
        p_src = p_own.at[g] if fresh else p_all.at[g, slot_from, odd]
        out = []
        for which, (src, dst) in enumerate(((c_src, c_all.at[rows, slot_to, odd]), (p_src, p_all.at[g, slot_to, odd]))):
            at = (kind, g, which)
            out.append(pltpu.make_async_remote_copy(src, dst, send_sem.at[at], recv_sem.at[at], device_id={"tp": peer}, device_id_type=MESH))
        return out

    def keep(g):
        rows = pl.ds(g * per, per)
        return [
            pltpu.make_async_copy(c_own.at[rows], c_all.at[rows, 0, odd], keep_sem.at[0, g]),
            pltpu.make_async_copy(p_own.at[g], p_all.at[g, 0, odd], keep_sem.at[1, g]),
            pltpu.make_async_copy(cq_own.at[rows], cq_pair.at[odd, rows], keep_sem.at[2, g]),
        ]

    def send_cq(g):
        rows = pl.ds(g * per, per)
        return pltpu.make_async_remote_copy(
            cq_own.at[rows], cq_pair.at[odd, rows], send_sem.at[7, g, 0], recv_sem.at[7, g, 0], device_id={"tp": other}, device_id_type=MESH
        )

    started = []

    def go(list_of_copies):
        for copy in list_of_copies:
            copy.start()
        started.extend(list_of_copies)

    load_x = [loads[0]] + loads[2 : 1 + groups]
    for g in range(groups):
        load_x[g].wait()
        if g == 0:
            loads[1].wait()
        x = x_buf[g * per : (g + 1) * per].reshape(per * toks, dim).astype(F32)
        a = (unit(x) * g1_ref[...]).astype(BF16)
        a_buf[g] = a
        kv = dot_t(a, wkv[...])
        c_own[g * per : (g + 1) * per] = (unit(kv[:, :rank]) * gkv_ref[...]).astype(BF16).reshape(per, toks, rank)
        turned = []
        for s in range(per):
            lanes = pl.ds(pl.multiple_of(chip * BLOCK, BLOCK), BLOCK)
            cos_pair, sin_pair = cos_ref[g * per + s, :, lanes], sin_ref[g * per + s, :, lanes]
            cos = jnp.where(odd == 1, cos_pair[:, toks:], cos_pair[:, :toks])
            sin = jnp.where(odd == 1, sin_pair[:, toks:], sin_pair[:, :toks])
            table = jnp.concatenate([cos, cos, -sin, sin], axis=0).T
            p = kv[s * toks : (s + 1) * toks, rank:]
            swapped = jnp.concatenate([p[:, half:], p[:, :half]], axis=1)
            turned.append(p * table[:, :rope] + swapped * table[:, rope:])
        p_own[g] = jnp.concatenate(turned, axis=1).astype(BF16)
        go(copies(g, 0, 1, 0, right, True) + copies(g, 0, 3, 1, left, True) + copies(g, 0, 0, 3, other, True))
        for copy in keep(g)[:2]:
            copy.start()

    loads[-1].wait()
    for g in range(groups):
        h = dot(a_buf[g], wdq[...])
        cq_own[g * per : (g + 1) * per] = (unit(h) * gq_ref[...]).astype(BF16).reshape(per, toks, h.shape[-1])
        go([send_cq(g)])
        keep(g)[2].start()

    for g in range(groups):
        for copy in copies(g, 0, 1, 0, right, True):
            copy.wait_recv()
        go(copies(g, 1, 1, 4, other))

        @pl.when(odd == 0)
        def _():
            for copy in copies(g, 1, 2, 2, right):
                copy.start()

        for copy in copies(g, 0, 3, 1, left, True):
            copy.wait_recv()
        go(copies(g, 3, 3, 5, other))

        @pl.when(odd == 1)
        def _():
            for copy in copies(g, 3, 2, 2, left):
                copy.start()

    for g in range(groups):
        for copy in copies(g, 1, 2, 2, right):
            copy.wait_recv()
        go(copies(g, 2, 2, 6, other))

    for g in range(groups):
        for kind, slot in ((3, 0), (4, 1), (5, 3), (6, 2)):
            for copy in copies(g, slot, slot, kind, other, slot == 0):
                copy.wait_recv()
        send_cq(g).wait_recv()
        for copy in copies(g, 1, 2, 2, right):
            copy.wait_send()
        for copy in keep(g):
            copy.wait()
    for copy in started:
        copy.wait_send()


def cache_kernel(len_ref, c_ref, p_ref, lat_ref, pe_ref, lat_out, pe_out, fresh, fresh_pe):
    step = pl.program_id(0)
    chip = lax.axis_index("tp") // 2
    per, slots, _, toks, rank = c_ref.shape
    rope = pe_ref.shape[1]
    cache_len = lat_ref.shape[1]
    chunk = slots * 2 * toks
    words = rank // BLOCK
    tile_row = lax.broadcasted_iota(jnp.int32, (16, BLOCK), 0)

    def slot_of(j):
        return lax.rem(chip - j + slots, slots)

    def one_sequence(s, _):
        length = len_ref[step * per + s]
        for j in range(slots):
            piece = c_ref[s, slot_of(j)].reshape(2 * toks, rank).astype(F32)
            for w in range(words):
                fresh[w, BLOCK + j * 2 * toks : BLOCK + (j + 1) * 2 * toks] = piece[:, w * BLOCK : (w + 1) * BLOCK]
        lat_out[s] = lat_ref[s]
        base = (length // 16) * 16
        skew = length - base

        def tile(k, partial):
            at = pl.multiple_of(base + k * 16, 16)
            for w in range(words):
                moved = fresh[w, pl.ds(BLOCK - skew + k * 16, 16), :].astype(BF16)
                cols = slice(w * BLOCK, (w + 1) * BLOCK)
                if partial:
                    local = tile_row + k * 16 - skew
                    moved = jnp.where((local >= 0) & (local < chunk), moved.astype(F32), lat_ref[s, pl.ds(at, 16), cols].astype(F32)).astype(BF16)
                lat_out[s, pl.ds(at, 16), cols] = moved

        for k in range(chunk // 16):
            tile(k, k == 0)
        pl.when(skew > 0)(functools.partial(tile, chunk // 16, True))
        return 0

    lax.fori_loop(0, per, one_sequence, 0)

    for j in range(slots):
        fresh_pe[cache_len - chunk + j * 2 * toks : cache_len - chunk + (j + 1) * 2 * toks] = p_ref[0, slot_of(j)].reshape(2 * toks, BLOCK).astype(F32)
    old = pe_ref[...].reshape(per * rope, cache_len).astype(F32)
    lane_seq = lax.broadcasted_iota(jnp.int32, (BLOCK, BLOCK), 1) // rope
    row = lax.broadcasted_iota(jnp.int32, (BLOCK, BLOCK), 0)
    for b in range(cache_len // BLOCK):
        value = old[:, b * BLOCK : (b + 1) * BLOCK].T
        for s in range(per):
            length = len_ref[step * per + s]
            moved = fresh_pe[pl.ds(b * BLOCK + cache_len - chunk - length, BLOCK), :]
            local = row + (b * BLOCK - length)
            value = jnp.where((lane_seq == s) & (local >= 0) & (local < chunk), moved, value)
        pe_out[:, :, b * BLOCK : (b + 1) * BLOCK] = value.T.astype(BF16).reshape(per, rope, BLOCK)


def attend_kernel(
    sizes,
    len_ref,
    w0_ref,
    w1_ref,
    w2a_ref,
    w2b_ref,
    w3_ref,
    cq_ref,
    cos_ref,
    sin_ref,
    c_ref,
    p_ref,
    lat_ref,
    pe_ref,
    own_ref,
    send_ref,
    qraw,
    qbd,
    rows,
    rot,
    kbuf,
    vbuf,
    s_bufs,
    p_bufs,
    obuf,
):
    heads, nope, rope, q_rank, rank = sizes
    step = pl.program_id(0)
    me = lax.axis_index("tp")
    chip, odd = me // 2, lax.rem(me, 2)
    seqs, chunk, _ = c_ref.shape
    per = pe_ref.shape[0]
    prefix_max = pe_ref.shape[2]
    toks = own_ref.shape[1]
    half = rope // 2
    head = nope + rope
    q_rows = heads * head
    slots = chunk // BLOCK
    pairs = slots * heads // 2
    quads = pairs // 2
    wide = 2 * BLOCK
    factor = LOG2E * head**-0.5
    cut = w2a_ref.shape[0]
    new_rows = pl.multiple_of((chip + 1) * BLOCK, BLOCK)

    def weight_rows(slot, start, count):
        if slot != 2:
            return (w0_ref, w1_ref, None, w3_ref)[slot][start : start + count]
        if start + count <= cut:
            return w2a_ref[start : start + count]
        if start >= cut:
            return w2b_ref[start - cut : start - cut + count]
        return jnp.concatenate([w2a_ref[start:cut], w2b_ref[0 : start + count - cut]], axis=0)

    def head_rows(first, count, base):
        parts = []
        for h in range(first, first + count):
            parts.append(weight_rows(h // heads, base + (h % heads) * nope, nope))
        return jnp.concatenate(parts, axis=0)

    @pl.when(step == 0)
    def _():
        qbd[...] = jnp.zeros_like(qbd)

    ring = qbd.shape[0]
    first_slot = lax.rem(step * seqs, ring)

    @pl.when(first_slot == 0)
    def _():
        rot[:chunk] = p_ref[0]
        old = pe_ref[...].reshape(per * rope, prefix_max).astype(F32)
        for b in range(prefix_max // BLOCK):
            rot[pl.ds(new_rows + b * BLOCK, BLOCK), :] = old[:, b * BLOCK : (b + 1) * BLOCK].T.astype(BF16)

    cq = jnp.concatenate([cq_ref[c, s] for s in range(seqs) for c in range(2)], axis=0)
    lanes_chip = pl.ds(pl.multiple_of(chip * BLOCK, BLOCK), BLOCK)
    for slot in range(slots):
        raw = qraw.at[slot % 2]
        total = None
        for k in range(q_rank // rank):
            part = dot_t(weight_rows(slot, k * q_rows, q_rows), cq[:, k * rank : (k + 1) * rank])
            total = part if total is None else total + part
        raw[...] = total
        for h in range(heads):
            index = slot * heads + h
            pair, side = index // 2, index % 2
            base = h * head
            cols = slice(side * BLOCK, (side + 1) * BLOCK)
            for s in range(seqs):
                lanes = slice(s * BLOCK, (s + 1) * BLOCK)
                at = first_slot + s
                qbd[at, pair, side * nope : (side + 1) * nope, cols] = raw[base : base + nope, lanes].astype(BF16)
                lo = raw[base + nope : base + nope + half, lanes]
                hi = raw[base + nope + half : base + head, lanes]
                cos, sin = cos_ref[s, :, lanes_chip], sin_ref[s, :, lanes_chip]
                lo, hi = lo * cos - hi * sin, hi * cos + lo * sin
                start = pl.multiple_of(BLOCK + at * rope, rope)
                qbd[at, pair, pl.ds(start, rope), cols] = jnp.concatenate([lo, hi], axis=0).astype(BF16)

    def one_sequence(s, _):
        length = len_ref[step * seqs + s]
        prefix_blocks = (length + BLOCK - 1) // BLOCK
        count = prefix_blocks + chip + 1
        at = first_slot + s
        rows[:chunk] = c_ref[s]
        rows[pl.ds(new_rows, prefix_max), :] = lat_ref[s]

        def attend(blocks):
            t = blocks * BLOCK
            lane = lax.broadcasted_iota(jnp.int32, (BLOCK, wide), 1) % BLOCK
            row = lax.broadcasted_iota(jnp.int32, (BLOCK, wide), 0)
            near = row <= lane
            tail = row < length - (prefix_blocks - 1) * BLOCK

            def keys_values(j):
                kbuf[j, :t] = dot_t(rows[:t], head_rows(4 * j, 4, (q_rank // rank) * q_rows)).astype(BF16)
                vbuf[j, :, :t] = dot_t(head_rows(4 * j, 4, (q_rank // rank) * q_rows + heads * nope), rows[:t]).astype(BF16)

            def score(pair):
                out = s_bufs[pair % 3]
                keys = jnp.concatenate([kbuf[pair // 2, :t, (pair % 2) * BLOCK : (pair % 2 + 1) * BLOCK], rot[:t]], axis=1)
                value = dot(keys, qbd[at, pair])
                most = None
                for b in range(blocks):
                    part = value[b * BLOCK : (b + 1) * BLOCK]
                    if b == 0:
                        part = jnp.where(near, part, NEVER)
                    if b == blocks - 1:
                        part = jnp.where(tail, part, NEVER)
                    out[b * BLOCK : (b + 1) * BLOCK] = part
                    part = jnp.max(part.reshape(BLOCK // 8, 8, wide), axis=0)
                    most = part if most is None else jnp.maximum(most, part)
                return jnp.max(most, axis=0, keepdims=True)

            def mix(pair, most):
                source, probs = s_bufs[pair % 3], p_bufs[pair % 2]
                total = None
                for b in range(blocks):
                    e = jnp.exp2((source[b * BLOCK : (b + 1) * BLOCK] - most) * factor)
                    part = jnp.sum(e.reshape(BLOCK // 8, 8, wide), axis=0)
                    total = part if total is None else total + part
                    probs[b * BLOCK : (b + 1) * BLOCK] = e.astype(BF16)
                inv = 1.0 / jnp.sum(total, axis=0, keepdims=True)
                value = vbuf[pair // 2, (pair % 2) * BLOCK : (pair % 2 + 1) * BLOCK, :t]
                o = dot(value, probs[:t]) * inv
                obuf[pair, :nope] = o[:nope, :BLOCK].astype(BF16)
                obuf[pair, nope:] = o[nope:, BLOCK:].astype(BF16)

            keys_values(0)
            most = {0: score(0), 1: score(1)}
            for pair in range(pairs):
                if pair % 2 == 0 and pair // 2 + 1 < quads:
                    keys_values(pair // 2 + 1)
                if pair + 2 < pairs:
                    most[pair + 2] = score(pair + 2)
                mix(pair, most.pop(pair))

        for blocks in range(2, (chunk + prefix_max) // BLOCK + 1):
            pl.when(count == blocks)(functools.partial(attend, blocks))

        for pair in range(pairs):
            o = obuf[pair].astype(F32).T.astype(BF16)
            cols = slice(pair * BLOCK, (pair + 1) * BLOCK)
            first, second = o[:toks], o[toks:]
            own_ref[s, :, cols] = jnp.where(odd == 1, second, first)
            send_ref[s, :, cols] = jnp.where(odd == 1, first, second)
        return 0

    lax.fori_loop(0, seqs, one_sequence, 0)


def output_kernel(own_ref, other_ref, *refs):
    *w_refs, x_ref, y_ref = refs
    seqs, toks, depth = own_ref.shape
    n = len(w_refs) // 2
    y = x_ref[...].reshape(seqs * toks, x_ref.shape[2]).astype(F32)
    for o, ws in ((own_ref, w_refs[:n]), (other_ref, w_refs[n:])):
        w = jnp.concatenate([r[...] for r in ws], axis=0)
        y = y + dot(o[...].reshape(seqs * toks, depth), w)
    y_ref[...] = y.astype(BF16).reshape(y_ref.shape)


def solution(mesh):
    size = mesh.shape["tp"]
    swap = [(i, i ^ 1) for i in range(size)]
    rightward = [(i, (i + 2) % size) for i in range(size)]
    leftward = [(i, (i - 2) % size) for i in range(size)]

    def ring(w):
        from_left = lax.ppermute(w, "tp", rightward)
        from_right = lax.ppermute(w, "tp", leftward)
        cut = w.shape[0] // 2
        return [w, from_left, lax.ppermute(from_left[:cut], "tp", rightward), lax.ppermute(from_right[cut:], "tp", leftward), from_right]

    def local_step(hidden, lengths, rope_cos, rope_sin, cache_lat, cache_pe, norm_in, w_dq, norm_q, w_dkv, norm_kv, w_uq, w_uk, w_uv, w_out):
        seqs, toks, dim = hidden.shape
        q_rank = w_dq.shape[1]
        rank, heads, nope = w_uk.shape
        rope = cache_pe.shape[2]
        cache_len = cache_lat.shape[1]
        chips = size // 2
        head = nope + rope
        pairs = chips * heads // 2
        depth = pairs * 2 * nope
        chunk = size * toks
        per = BLOCK // rope
        groups = seqs // per
        cos_t, sin_t = rope_cos.transpose(0, 2, 1), rope_sin.transpose(0, 2, 1)
        pe_t = cache_pe.transpose(0, 2, 1)
        wkv_down = w_dkv.transpose(1, 0)

        wq = w_uq.transpose(1, 2, 0).reshape(heads * head, q_rank)
        weights = [wq[:, k * rank : (k + 1) * rank] for k in range(q_rank // rank)]
        weights += [w.transpose(1, 2, 0).reshape(heads * nope, rank) for w in (w_uk, w_uv)]
        weights = ring(jnp.concatenate(weights, axis=0))

        any_spec = pl.BlockSpec(memory_space=pl.ANY)
        vmem_spec = pl.BlockSpec(memory_space=pltpu.VMEM)
        c_all, p_all, cq_pair = pl.pallas_call(
            functools.partial(project_kernel, size),
            in_specs=[any_spec, vmem_spec, any_spec, vmem_spec, any_spec, vmem_spec, vmem_spec, vmem_spec],
            out_specs=[any_spec] * 3,
            out_shape=[
                jax.ShapeDtypeStruct((seqs, chips, 2, toks, rank), BF16),
                jax.ShapeDtypeStruct((groups, chips, 2, toks, BLOCK), BF16),
                jax.ShapeDtypeStruct((2, seqs, toks, q_rank), BF16),
            ],
            scratch_shapes=[
                pltpu.VMEM(hidden.shape, BF16),
                pltpu.VMEM(w_dq.shape, BF16),
                pltpu.VMEM(wkv_down.shape, BF16),
                pltpu.VMEM((groups, per * toks, dim), BF16),
                pltpu.VMEM((seqs, toks, rank), BF16),
                pltpu.VMEM((groups, toks, BLOCK), BF16),
                pltpu.VMEM((seqs, toks, q_rank), BF16),
                pltpu.SemaphoreType.DMA((groups + 2,)),
                pltpu.SemaphoreType.DMA((3, groups)),
                pltpu.SemaphoreType.DMA((8, groups, 2)),
                pltpu.SemaphoreType.DMA((8, groups, 2)),
            ],
            compiler_params=pltpu.CompilerParams(collective_id=0, has_side_effects=True, vmem_limit_bytes=40 * MIB),
            cost_estimate=pl.CostEstimate(flops=2 * seqs * toks * dim * (q_rank + rank + rope), bytes_accessed=12 * MIB, transcendentals=0),
            name="project",
        )(hidden, norm_in, w_dq, norm_q, wkv_down, norm_kv, cos_t, sin_t)

        w_out, c_all = lax.optimization_barrier((w_out, c_all))
        out_own = ring(w_out)
        out_other = [lax.ppermute(w, "tp", swap) for w in out_own]

        lat_new, pe_new = pl.pallas_call(
            cache_kernel,
            grid_spec=pltpu.PrefetchScalarGridSpec(
                num_scalar_prefetch=1,
                grid=(groups,),
                in_specs=[
                    pl.BlockSpec((per, chips, 2, toks, rank), lambda i, n: (i, 0, 0, 0, 0)),
                    pl.BlockSpec((1, chips, 2, toks, BLOCK), lambda i, n: (i, 0, 0, 0, 0)),
                    pl.BlockSpec((per, cache_len, rank), lambda i, n: (i, 0, 0)),
                    pl.BlockSpec((per, rope, cache_len), lambda i, n: (i, 0, 0)),
                ],
                out_specs=[
                    pl.BlockSpec((per, cache_len, rank), lambda i, n: (i, 0, 0)),
                    pl.BlockSpec((per, rope, cache_len), lambda i, n: (i, 0, 0)),
                ],
                scratch_shapes=[
                    pltpu.VMEM((rank // BLOCK, chunk + 2 * BLOCK, BLOCK), F32),
                    pltpu.VMEM((2 * cache_len - chunk, BLOCK), F32),
                ],
            ),
            out_shape=[jax.ShapeDtypeStruct(cache_lat.shape, BF16), jax.ShapeDtypeStruct(pe_t.shape, BF16)],
            cost_estimate=pl.CostEstimate(flops=4 * 10**9, bytes_accessed=20 * MIB, transcendentals=0),
            name="cache",
        )(lengths, c_all, p_all, cache_lat, pe_t)

        step = 2
        prefix = cache_len - chunk
        whole = lambda a: pl.BlockSpec(a.shape, lambda i, n: (0,) * a.ndim, pipeline_mode=pl.Buffered(1))
        o_shape = jax.ShapeDtypeStruct((seqs, toks, depth), BF16)
        own, send = pl.pallas_call(
            functools.partial(attend_kernel, (heads, nope, rope, q_rank, rank)),
            grid_spec=pltpu.PrefetchScalarGridSpec(
                num_scalar_prefetch=1,
                grid=(seqs // step,),
                in_specs=[whole(w) for w in weights]
                + [
                    pl.BlockSpec((2, step, toks, q_rank), lambda i, n: (0, i, 0, 0)),
                    pl.BlockSpec((step, rope // 2, chunk), lambda i, n: (i, 0, 0)),
                    pl.BlockSpec((step, rope // 2, chunk), lambda i, n: (i, 0, 0)),
                    pl.BlockSpec((step, chunk, rank), lambda i, n: (i, 0, 0)),
                    pl.BlockSpec((1, chunk, BLOCK), lambda i, n: (i * step // per, 0, 0)),
                    pl.BlockSpec((step, prefix, rank), lambda i, n: (i, 0, 0)),
                    pl.BlockSpec((per, rope, prefix), lambda i, n: (i * step // per, 0, 0)),
                ],
                out_specs=[
                    pl.BlockSpec((step, toks, depth), lambda i, n: (i, 0, 0)),
                    pl.BlockSpec((step, toks, depth), lambda i, n: (i, 0, 0)),
                ],
                scratch_shapes=[
                    pltpu.VMEM((2, heads * head, step * BLOCK), F32),
                    pltpu.VMEM((per, pairs, 2 * BLOCK, 2 * BLOCK), BF16),
                    pltpu.VMEM((cache_len, rank), BF16),
                    pltpu.VMEM((cache_len, BLOCK), BF16),
                    pltpu.VMEM((pairs // 2, cache_len, 2 * BLOCK), BF16),
                    pltpu.VMEM((pairs // 2, 2 * BLOCK, cache_len), BF16),
                    [pltpu.VMEM((cache_len, 2 * BLOCK), F32) for _ in range(3)],
                    [pltpu.VMEM((cache_len, 2 * BLOCK), BF16) for _ in range(2)],
                    pltpu.VMEM((pairs, BLOCK, BLOCK), BF16),
                ],
            ),
            out_shape=[o_shape, o_shape],
            compiler_params=pltpu.CompilerParams(vmem_limit_bytes=60 * MIB),
            cost_estimate=pl.CostEstimate(flops=40 * 10**9, bytes_accessed=30 * MIB, transcendentals=30 * 10**6),
            name="attend",
        )(
            lengths,
            *weights,
            cq_pair,
            cos_t,
            sin_t,
            c_all.reshape(seqs, chunk, rank),
            p_all.reshape(groups, chunk, BLOCK),
            cache_lat,
            pe_t,
        )

        other = lax.ppermute(send, "tp", swap)

        wide = 512
        held = lambda a: pl.BlockSpec(a.shape, lambda i: (0,) * a.ndim, pipeline_mode=pl.Buffered(1))
        y = pl.pallas_call(
            output_kernel,
            grid=(dim // wide,),
            in_specs=[held(own), held(other)]
            + [pl.BlockSpec((w.shape[0], wide), lambda i: (0, i)) for w in out_own + out_other]
            + [pl.BlockSpec((seqs, toks, wide), lambda i: (0, 0, i))],
            out_specs=pl.BlockSpec((seqs, toks, wide), lambda i: (0, 0, i)),
            out_shape=jax.ShapeDtypeStruct(hidden.shape, BF16),
            cost_estimate=pl.CostEstimate(flops=2 * seqs * toks * dim * dim, bytes_accessed=30 * MIB, transcendentals=0),
            name="output",
        )(own, other, *out_own, *out_other, hidden)
        return y, lat_new, pe_new.transpose(0, 2, 1)

    spec_tok = P("dp", "tp", None)
    spec_len = P("dp")
    spec_seq = P("dp", None, None)
    spec_vec = P(None)
    spec_mat = P(None, None)
    spec_head = P(None, "tp", None)
    spec_rows = P("tp", None)
    in_specs = (spec_tok, spec_len, spec_seq, spec_seq, spec_seq, spec_seq, spec_vec, spec_mat, spec_vec, spec_mat, spec_vec, spec_head, spec_head, spec_head, spec_rows)
    return jax.shard_map(local_step, mesh=mesh, in_specs=in_specs, out_specs=(spec_tok, spec_seq, spec_seq), check_vma=False)
```

time: 1030 us -> 191 us (0.19)
  waiting for transfers between devices: 450 us -> 41.5 us
  matrix products: 282 us -> 0 us
  other arithmetic: 168 us -> 0 us
  Pallas kernels: 0 us -> 104 us
  local copies, waits for them, and re-layouts: 108 us -> 13.5 us
  starting transfers between devices: 0.13 us -> 31.6 us
  between operations: 14.2 us -> 0.86 us
    reduce_scatter x1 -> x0, waiting for transfers between devices: 307 us -> none  [local_step(): reduced = lax.psum_scatter(head_sum, 'tp', scatter_dimension=1, tiled=True)]
    dot_general x7 -> x0, matrix products: 187 us -> none  [the longest x1 48 us: local_step(): jnp.einsum('bthd,bshd->bhts', q_nope, keys_nope, preferred_element_type=j...]
    all_gather x1 -> x0, waiting for transfers between devices: 143 us -> none  [local_step(): gathered = lax.all_gather(hidden, 'tp', axis=1, tiled=True)]
    scatter x49 -> x0, other arithmetic: 131 us -> none
    pallas_call x0 -> x4, Pallas kernels: none -> 104 us  [the longest x1 50 us: local_step(): pl.pallas_call(functools.partial(attend_kernel, (heads, nope, rope, q_ran...]
    scatter x96 -> x0, local copies, waits for them, and re-layouts: 96.4 us -> none
    sub x1 -> x0, matrix products: 95.6 us -> none  [local_step(): attn_probs = jax.nn.softmax(scores, axis=-1).astype(jnp.bfloat16)]
    ppermute x0 -> x14, waiting for transfers between devices: none -> 41.5 us  [the longest x2 22.2 us: ring(): from_right = lax.ppermute(w, 'tp', leftward)]
  transfers between devices with their start and end apart: 2 -> 14, of which waited for: 2 -> 3; matrix products, arithmetic and copies ran while one was open for 1% -> 0% of each run, Pallas kernels for 0% -> 46%
where the time goes in v2:
time: 191 us
  Pallas kernels  104 us (54%)
  waiting for transfers between devices  41.5 us (22%)
  starting transfers between devices  31.6 us (17%)
  local copies, waits for them, and re-layouts  13.5 us (7%)
    pallas_call x1, Pallas kernels, local_step(): pl.pallas_call(functools.partial(attend_kernel, (heads, nope, rope, q_ran...  50 us
    pallas_call x1, Pallas kernels, local_step(): pl.pallas_call(functools.partial(project_kernel, size), in_specs=[any_spe...  27.6 us
    ppermute x2, starting transfers between devices, ring(): lax.ppermute(from_right[cut:], 'tp', leftward)  22.3 us
    ppermute x2, waiting for transfers between devices, ring(): from_right = lax.ppermute(w, 'tp', leftward)  22.2 us
    ppermute x2, waiting for transfers between devices, ring(): lax.ppermute(from_right[cut:], 'tp', leftward)  16.7 us
    pallas_call x1, Pallas kernels, local_step(): pl.pallas_call(output_kernel, grid=(dim // wide,), in_specs=[held(own), h...  15.8 us
    unnamed x40, local copies, waits for them, and re-layouts  12.4 us
    pallas_call x1, Pallas kernels, local_step(): pl.pallas_call(cache_kernel, grid_spec=pltpu.PrefetchScalarGridSpec(num_s...  10.4 us
  transfers between devices with their start and end apart: 14, of which 3 were waited for; matrix products, arithmetic and copies ran while one was open for 0% of the time, Pallas kernels for 46%

profile of v2, /device:TPU:81, one launch (start us, length us, event | category | flops | bytes accessed | tf_op | source)
XLA Modules:
  0.0 191.3 jit_solution(15883356120472322245)
XLA Ops:
  0.7 1.1 slice_dynamic-update-slice_fusion.2
  1.8 1.2 slice_dynamic-update-slice_fusion.1
  3.0 1.0 slice_dynamic-update-slice_fusion
  4.0 0.9 constant_dynamic-update-slice_fusion.w0_ref
  5.0 3.8 %collective-permute-start.2 = (bf16[2080,256]{1,0:T(8,128)(2,1)S(1)}, bf16[2080,256]{1,0:T(8,128)(2,1)S(1)}, u32[]{:S(2)}, u32[]{:S(2)}) collective-permute-start(bf16[2080,256]{1,0:T(8,128)(2,1)S(1)} %constant_dynamic-update-slice_fusion.w0_ref), channel_id=1, source_target_pairs={{0,6},{1,7},{2,0},{3,1},{4,2},{5,3},{6,4},{7,5},{8,14},{9,15},{10,... | collective-permute-start | bytes 3194888 | tf_op jit(solution)/shard_map/ppermute | solution.py:428
  8.8 22.2 %collective-permute-done.2.w3_ref = bf16[2080,256]{1,0:T(8,128)(2,1)S(1)} collective-permute-done((bf16[2080,256]{1,0:T(8,128)(2,1)S(1)}, bf16[2080,256]{1,0:T(8,128)(2,1)S(1)}, u32[]{:S(2)}, u32[]{:S(2)}) %collective-permute-start.2) | collective-permute-done | bytes 1064992 | tf_op jit(solution)/shard_map/ppermute | solution.py:428
  31.0 3.5 %collective-permute-start.3 = (bf16[1040,256]{1,0:T(8,128)(2,1)S(1)}, bf16[1040,256]{1,0:T(8,128)(2,1)S(1)}, u32[]{:S(2)}, u32[]{:S(2)}) collective-permute-start(bf16[1040,256]{1,0:T(8,128)(2,1)S(1)} %slice.32), channel_id=1, source_target_pairs={{0,6},{1,7},{2,0},{3,1},{4,2},{5,3},{6,4},{7,5},{8,14},{9,15},{10,... | collective-permute-start | bytes 1597448 | tf_op jit(solution)/shard_map/ppermute | solution.py:430
  34.6 0.1 collective-permute-start.1
  34.7 0.9 copy-done.13
  35.6 1.4 copy-done.1
  37.0 1.0 copy-done.2
  38.0 1.0 copy-done.3
  39.0 27.6 %project.1 = (bf16[12,4,2,64,256]{4,3,2,1,0:T(8,128)(2,1)S(1)}, bf16[3,4,2,64,128]{4,3,2,1,0:T(8,128)(2,1)S(1)}, bf16[2,12,64,768]{3,2,1,0:T(8,128)(2,1)S(1)}) custom-call(bf16[12,64,2560]{2,1,0:T(8,128)(2,1)S(1)} %copy-done, f32[2560]{0:T(1024)S(1)} %copy-done.4, bf16[2560,768]{1,0:T(8,128)(2,1)} %wdq_hbm.1, f32[768]{0:T(1024)S(1)} %copy-done.5, ...), custom_call_target="tpu_custom_call" | custom-call | flops 4152360960 | bytes 12582912 | tf_op jit(solution)/shard_map/project/pallas_call | solution.py:456
  66.6 1.7 copy-done.7
  68.2 0.8 copy-done.8
  69.0 1.4 copy-done.9
  70.4 0.1 collective-permute-start.9
  70.5 1.5 collective-permute-start.5
  72.0 0.8 copy-done.17
  72.8 0.2 copy-done.16
  73.0 50.0 %attend.1 = (bf16[12,64,1280]{2,1,0:T(8,128)(2,1)}, bf16[12,64,1280]{2,1,0:T(8,128)(2,1)}) custom-call(s32[12]{0:T(128)} %len_ref.3, bf16[2080,256]{1,0:T(8,128)(2,1)} %copy-done.15, bf16[2080,256]{1,0:T(8,128)(2,1)} %copy-done.13, bf16[1040,256]{1,0:T(8,128)(2,1)} %copy-done.17, bf16[1040,256]{1,0:T(8,128)(2,1)} %copy-done.16, ...), custom_call_target="tpu_custom_call" | custom-call | flops 40000000000 | bytes 31457280 | tf_op jit(solution)/shard_map/attend/pallas_call | solution.py:516
  123.0 1.1 collective-permute-start.4
  124.2 18.8 %collective-permute-start.8 = (bf16[160,2560]{1,0:T(8,128)(2,1)S(1)}, bf16[160,2560]{1,0:T(8,128)(2,1)}, u32[]{:S(2)}, u32[]{:S(2)}) collective-permute-start(bf16[160,2560]{1,0:T(8,128)(2,1)S(1)} %slice.34), channel_id=1, source_target_pairs={{0,6},{1,7},{2,0},{3,1},{4,2},{5,3},{6,4},{7,5},{8,14},{9,15},{10,... | collective-permute-start | bytes 2457608 | tf_op jit(solution)/shard_map/ppermute | solution.py:430
  143.1 0.1 collective-permute-start.6
  143.2 0.4 collective-permute-start.13
  143.6 0.2 collective-permute-start.10
  143.8 16.7 %collective-permute-done.8.refs_3_ = bf16[160,2560]{1,0:T(8,128)(2,1)} collective-permute-done((bf16[160,2560]{1,0:T(8,128)(2,1)S(1)}, bf16[160,2560]{1,0:T(8,128)(2,1)}, u32[]{:S(2)}, u32[]{:S(2)}) %collective-permute-start.8) | collective-permute-done | bytes 819232 | tf_op jit(solution)/shard_map/ppermute | solution.py:430
  160.6 0.9 collective-permute-start.12
  161.5 2.5 %collective-permute-done.6.refs_2_ = bf16[160,2560]{1,0:T(8,128)(2,1)} collective-permute-done((bf16[160,2560]{1,0:T(8,128)(2,1)S(1)}, bf16[160,2560]{1,0:T(8,128)(2,1)}, u32[]{:S(2)}, u32[]{:S(2)}) %collective-permute-start.6) | collective-permute-done | bytes 819232 | tf_op jit(solution)/shard_map/ppermute | solution.py:430
  164.0 1.1 collective-permute-start.11
  165.1 10.4 %cache.1 = (bf16[12,1024,256]{2,1,0:T(8,128)(2,1)}, bf16[12,32,1024]{2,1,0:T(8,128)(2,1)}) custom-call(s32[12]{0:T(128)} %len_ref.3, bf16[12,4,2,64,256]{4,3,2,1,0:T(8,128)(2,1)} %copy-done.7, bf16[3,4,2,64,128]{4,3,2,1,0:T(8,128)(2,1)} %copy-done.8, bf16[12,1024,256]{2,1,0:T(8,128)(2,1)} %lat_ref.3, bf16[12,32,1024]{2,1,0:T(8,128)(2,1)} %bitcast.29), custom_call_target="tpu_custom_call" | custom-call | flops 4000000000 | bytes 20971520 | tf_op jit(solution)/shard_map/cache/pallas_call | solution.py:487
  175.5 15.8 %output.1 = bf16[12,64,2560]{2,1,0:T(8,128)(2,1)} custom-call(bf16[12,64,1280]{2,1,0:T(8,128)(2,1)} %get-tuple-element.16.own_ref, bf16[12,64,1280]{2,1,0:T(8,128)(2,1)} %collective-permute-done.4.other_ref, bf16[320,2560]{1,0:T(8,128)(2,1)} %refs_0_, bf16[320,2560]{1,0:T(8,128)(2,1)} %copy-done.11, bf16[160,2560]{1,0:T(8,128)(2,1)} %collective-permute-done.6.refs_2_, ...), custom_call_target="tpu_custom_call" | custom-call | flops 10066329600 | bytes 31457280 | tf_op jit(solution)/shard_map/output/pallas_call | solution.py:567
  (45 shorter events, 0.3 us)
Async XLA Ops:
  0.6 3.4 %copy-start.14 = (bf16[256,5,64]{0,2,1:T(8,128)(2,1)S(1)}, bf16[256,5,64]{0,2,1:T(8,128)(2,1)}, u32[]{:S(2)}) copy-start(bf16[256,5,64]{0,2,1:T(8,128)(2,1)} %param.27) | copy-start | bytes 491524
  0.6 35.0 %copy-start = (bf16[12,64,2560]{2,1,0:T(8,128)(2,1)S(1)}, bf16[12,64,2560]{2,1,0:T(8,128)(2,1)}, u32[]{:S(2)}) copy-start(bf16[12,64,2560]{2,1,0:T(8,128)(2,1)} %refs_10_.1) | copy-start | bytes 11796484
  3.9 31.7 %copy-start.4 = (f32[2560]{0:T(1024)S(1)}, f32[2560]{0:T(1024)}, u32[]{:S(2)}) copy-start(f32[2560]{0:T(1024)} %g1_ref.1) | copy-start | bytes 30724
  4.0 31.7 %copy-start.5 = (f32[768]{0:T(1024)S(1)}, f32[768]{0:T(1024)}, u32[]{:S(2)}) copy-start(f32[768]{0:T(1024)} %gq_ref.1) | copy-start | bytes 9220
  4.0 31.7 %copy-start.6 = (f32[256]{0:T(256)S(1)}, f32[256]{0:T(256)}, u32[]{:S(2)}) copy-start(f32[256]{0:T(256)} %gkv_ref.1) | copy-start | bytes 3076
  4.9 29.8 %copy-start.15 = (bf16[2080,256]{1,0:T(8,128)(2,1)}, bf16[2080,256]{1,0:T(8,128)(2,1)S(1)}, u32[]{:S(2)}) copy-start(bf16[2080,256]{1,0:T(8,128)(2,1)S(1)} %constant_dynamic-update-slice_fusion.w0_ref) | copy-start | bytes 3194884
  5.0 26.0 %collective-permute-start.2 = (bf16[2080,256]{1,0:T(8,128)(2,1)S(1)}, bf16[2080,256]{1,0:T(8,128)(2,1)S(1)}, u32[]{:S(2)}, u32[]{:S(2)}) collective-permute-start(bf16[2080,256]{1,0:T(8,128)(2,1)S(1)} %constant_dynamic-update-slice_fusion.w0_ref), channel_id=1, source_target_pairs={{0,6},{1,7},{2,0},{3,1},{4,2},{5,3},{6,4},{7,5},{8,14},{9,15},{10,... | collective-permute-start | bytes 3194888 | tf_op jit(solution)/shard_map/ppermute | solution.py:428
  8.8 25.8 %collective-permute-start = (bf16[2080,256]{1,0:T(8,128)(2,1)S(1)}, bf16[2080,256]{1,0:T(8,128)(2,1)S(1)}, u32[]{:S(2)}, u32[]{:S(2)}) collective-permute-start(bf16[2080,256]{1,0:T(8,128)(2,1)S(1)} %constant_dynamic-update-slice_fusion.w0_ref), channel_id=1, source_target_pairs={{0,2},{1,3},{2,4},{3,5},{4,6},{5,7},{6,0},{7,1},{8,10},{9,11},{10,... | collective-permute-start | bytes 3194888 | tf_op jit(solution)/shard_map/ppermute | solution.py:427
  31.0 3.7 %copy-start.12 = (bf16[2080,256]{1,0:T(8,128)(2,1)}, bf16[2080,256]{1,0:T(8,128)(2,1)S(1)}, u32[]{:S(2)}) copy-start(bf16[2080,256]{1,0:T(8,128)(2,1)S(1)} %collective-permute-done.2.w3_ref) | copy-start | bytes 3194884
  31.0 40.9 %collective-permute-start.3 = (bf16[1040,256]{1,0:T(8,128)(2,1)S(1)}, bf16[1040,256]{1,0:T(8,128)(2,1)S(1)}, u32[]{:S(2)}, u32[]{:S(2)}) collective-permute-start(bf16[1040,256]{1,0:T(8,128)(2,1)S(1)} %slice.32), channel_id=1, source_target_pairs={{0,6},{1,7},{2,0},{3,1},{4,2},{5,3},{6,4},{7,5},{8,14},{9,15},{10,... | collective-permute-start | bytes 1597448 | tf_op jit(solution)/shard_map/ppermute | solution.py:430
  34.6 1.1 copy-start.13
  34.6 37.3 %collective-permute-start.1 = (bf16[1040,256]{1,0:T(8,128)(2,1)S(1)}, bf16[1040,256]{1,0:T(8,128)(2,1)S(1)}, u32[]{:S(2)}, u32[]{:S(2)}) collective-permute-start(bf16[1040,256]{1,0:T(8,128)(2,1)S(1)} %slice.31), channel_id=1, source_target_pairs={{0,2},{1,3},{2,4},{3,5},{4,6},{5,7},{6,0},{7,1},{8,10},{9,11},{10,... | collective-permute-start | bytes 1597448 | tf_op jit(solution)/shard_map/ppermute | solution.py:430
  35.6 1.4 copy-start.1
  37.0 1.0 copy-start.2
  38.0 1.0 copy-start.3
  66.6 1.7 copy-start.7
  68.2 0.8 copy-start.8
  69.0 1.4 copy-start.9
  70.4 73.3 %collective-permute-start.9 = (bf16[320,2560]{1,0:T(8,128)(2,1)}, bf16[320,2560]{1,0:T(8,128)(2,1)}, u32[]{:S(2)}, u32[]{:S(2)}) collective-permute-start(bf16[320,2560]{1,0:T(8,128)(2,1)} %refs_0_), channel_id=1, source_target_pairs={{0,1},{1,0},{2,3},{3,2},{4,5},{5,4},{6,7},{7,6},{8,9},{9,8},{10,11... | collective-permute-start | bytes 4915208 | tf_op jit(solution)/shard_map/ppermute | solution.py:485
  70.5 53.7 %collective-permute-start.7 = (bf16[320,2560]{1,0:T(8,128)(2,1)}, bf16[320,2560]{1,0:T(8,128)(2,1)S(1)}, u32[]{:S(2)}, u32[]{:S(2)}) collective-permute-start(bf16[320,2560]{1,0:T(8,128)(2,1)} %refs_0_), channel_id=1, source_target_pairs={{0,6},{1,7},{2,0},{3,1},{4,2},{5,3},{6,4},{7,5},{8,14},{9,15},{10,... | collective-permute-start | bytes 4915208 | tf_op jit(solution)/shard_map/ppermute | solution.py:428
  70.5 72.6 %collective-permute-start.5 = (bf16[320,2560]{1,0:T(8,128)(2,1)}, bf16[320,2560]{1,0:T(8,128)(2,1)S(1)}, u32[]{:S(2)}, u32[]{:S(2)}) collective-permute-start(bf16[320,2560]{1,0:T(8,128)(2,1)} %refs_0_), channel_id=1, source_target_pairs={{0,2},{1,3},{2,4},{3,5},{4,6},{5,7},{6,0},{7,1},{8,10},{9,11},{10,... | collective-permute-start | bytes 4915208 | tf_op jit(solution)/shard_map/ppermute | solution.py:427
  71.9 1.0 copy-start.16
  71.9 0.8 copy-start.17
  123.0 52.5 %collective-permute-start.4 = (bf16[12,64,1280]{2,1,0:T(8,128)(2,1)}, bf16[12,64,1280]{2,1,0:T(8,128)(2,1)}, u32[]{:S(2)}, u32[]{:S(2)}) collective-permute-start(bf16[12,64,1280]{2,1,0:T(8,128)(2,1)} %get-tuple-element.17), channel_id=1, source_target_pairs={{0,1},{1,0},{2,3},{3,2},{4,5},{5,4},{6,7},{7,6},{8,9},{9,8},{10,11... | collective-permute-start | bytes 5898248 | tf_op jit(solution)/shard_map/ppermute | solution.py:563
  124.1 19.1 %copy-start.10 = (bf16[320,2560]{1,0:T(8,128)(2,1)}, bf16[320,2560]{1,0:T(8,128)(2,1)S(1)}, u32[]{:S(2)}) copy-start(bf16[320,2560]{1,0:T(8,128)(2,1)S(1)} %collective-permute-done.7.refs_4_) | copy-start | bytes 4915204
  124.2 36.4 %collective-permute-start.8 = (bf16[160,2560]{1,0:T(8,128)(2,1)S(1)}, bf16[160,2560]{1,0:T(8,128)(2,1)}, u32[]{:S(2)}, u32[]{:S(2)}) collective-permute-start(bf16[160,2560]{1,0:T(8,128)(2,1)S(1)} %slice.34), channel_id=1, source_target_pairs={{0,6},{1,7},{2,0},{3,1},{4,2},{5,3},{6,4},{7,5},{8,14},{9,15},{10,... | collective-permute-start | bytes 2457608 | tf_op jit(solution)/shard_map/ppermute | solution.py:430
  143.0 32.5 %copy-start.11 = (bf16[320,2560]{1,0:T(8,128)(2,1)}, bf16[320,2560]{1,0:T(8,128)(2,1)S(1)}, u32[]{:S(2)}) copy-start(bf16[320,2560]{1,0:T(8,128)(2,1)S(1)} %collective-permute-done.5.refs_1_) | copy-start | bytes 4915204
  143.1 20.9 %collective-permute-start.6 = (bf16[160,2560]{1,0:T(8,128)(2,1)S(1)}, bf16[160,2560]{1,0:T(8,128)(2,1)}, u32[]{:S(2)}, u32[]{:S(2)}) collective-permute-start(bf16[160,2560]{1,0:T(8,128)(2,1)S(1)} %slice.33), channel_id=1, source_target_pairs={{0,2},{1,3},{2,4},{3,5},{4,6},{5,7},{6,0},{7,1},{8,10},{9,11},{10,... | collective-permute-start | bytes 2457608 | tf_op jit(solution)/shard_map/ppermute | solution.py:430
  143.2 32.3 %collective-permute-start.13 = (bf16[320,2560]{1,0:T(8,128)(2,1)S(1)}, bf16[320,2560]{1,0:T(8,128)(2,1)}, u32[]{:S(2)}, u32[]{:S(2)}) collective-permute-start(bf16[320,2560]{1,0:T(8,128)(2,1)S(1)} %collective-permute-done.7.refs_4_), channel_id=1, source_target_pairs={{0,1},{1,0},{2,3},{3,2},{4,5},{5,4},{6,7},{7,6},{8,9},{9,8},{10,11... | collective-permute-start | bytes 4915208 | tf_op jit(solution)/shard_map/ppermute | solution.py:485
  143.6 31.9 %collective-permute-start.10 = (bf16[320,2560]{1,0:T(8,128)(2,1)S(1)}, bf16[320,2560]{1,0:T(8,128)(2,1)}, u32[]{:S(2)}, u32[]{:S(2)}) collective-permute-start(bf16[320,2560]{1,0:T(8,128)(2,1)S(1)} %collective-permute-done.5.refs_1_), channel_id=1, source_target_pairs={{0,1},{1,0},{2,3},{3,2},{4,5},{5,4},{6,7},{7,6},{8,9},{9,8},{10,11... | collective-permute-start | bytes 4915208 | tf_op jit(solution)/shard_map/ppermute | solution.py:485
  160.6 14.9 %collective-permute-start.12 = (bf16[160,2560]{1,0:T(8,128)(2,1)}, bf16[160,2560]{1,0:T(8,128)(2,1)}, u32[]{:S(2)}, u32[]{:S(2)}) collective-permute-start(bf16[160,2560]{1,0:T(8,128)(2,1)} %collective-permute-done.8.refs_3_), channel_id=1, source_target_pairs={{0,1},{1,0},{2,3},{3,2},{4,5},{5,4},{6,7},{7,6},{8,9},{9,8},{10,11... | collective-permute-start | bytes 2457608 | tf_op jit(solution)/shard_map/ppermute | solution.py:485
  164.0 11.5 %collective-permute-start.11 = (bf16[160,2560]{1,0:T(8,128)(2,1)}, bf16[160,2560]{1,0:T(8,128)(2,1)}, u32[]{:S(2)}, u32[]{:S(2)}) collective-permute-start(bf16[160,2560]{1,0:T(8,128)(2,1)} %collective-permute-done.6.refs_2_), channel_id=1, source_target_pairs={{0,1},{1,0},{2,3},{3,2},{4,5},{5,4},{6,7},{7,6},{8,9},{9,8},{10,11... | collective-permute-start | bytes 2457608 | tf_op jit(solution)/shard_map/ppermute | solution.py:485

commit v3 on v0

v3 whole, which is shorter than its diff:
```python
import functools

import jax
import jax.numpy as jnp
from jax import lax
from jax.experimental import pallas as pl
from jax.experimental.pallas import tpu as pltpu
from jax.sharding import PartitionSpec as P

BLOCK = 128
LOG2E = 1.4426950408889634
NEVER = -1e30
F32 = jnp.float32
BF16 = jnp.bfloat16
MESH = pl.DeviceIdType.MESH
MIB = 2**20


def dot(a, b):
    return lax.dot_general(a, b, (((1,), (0,)), ((), ())), preferred_element_type=F32)


def dot_t(a, b):
    return lax.dot_general(a, b, (((1,), (1,)), ((), ())), preferred_element_type=F32)


def unit(x):
    return x * lax.rsqrt(jnp.mean(x * x, axis=-1, keepdims=True) + 1e-6)


class Wire:
    def __init__(self, send_sem, recv_sem):
        self.sems = (send_sem, recv_sem)
        self.made = {}
        self.index = {}

    def add(self, name, src, dst, **peer):
        self.index[name] = len(self.index)
        self.made[name] = lambda: pltpu.make_async_remote_copy(
            src(), dst(), self.sems[0].at[self.index[name]], self.sems[1].at[self.index[name]], device_id=peer, device_id_type=MESH
        )

    def start(self, *names):
        for name in names:
            self.made[name]().start()

    def landed(self, *names):
        for name in names:
            self.made[name]().wait_recv()

    def sent(self, *names):
        for name in names:
            self.made[name]().wait_send()


def main_kernel(
    plan,
    len_ref,
    x_hbm,
    g1_ref,
    wdq_hbm,
    gq_ref,
    wdkv_hbm,
    gkv_ref,
    cos_ref,
    sin_ref,
    wq_hbm,
    wk_hbm,
    wv_hbm,
    wo_hbm,
    lat_hbm,
    pe_hbm,
    c_out,
    p_out,
    o_out,
    wo_out,
    x_buf,
    wdq,
    wdkv,
    a_buf,
    rows,
    rot,
    pe_buf,
    cq_buf,
    wq,
    wkv,
    kb,
    vb,
    qb,
    sb,
    mb,
    pb,
    lb,
    o_own,
    o_send,
    load_sem,
    send_sem,
    recv_sem,
):
    size, paired = plan
    me = lax.axis_index("tp")
    odd = lax.rem(me, 2)
    chip = me // 2
    right, left = lax.rem(me + 2, size), lax.rem(me + size - 2, size)
    onward = jnp.where(odd == 0, right, left)
    other = me + 1 - 2 * odd
    dp = lax.axis_index("dp")
    e = lax.rem(dp, 2) if paired else dp * 0
    partner = dp + 1 - 2 * e

    seqs, toks, dim = x_hbm.shape
    groups = rot.shape[0]
    per = seqs // groups
    rank = rows.shape[2]
    slots = size // 2
    chunk = size * toks
    prefix = rows.shape[1] - chunk
    heads = wq.shape[0] // slots
    head, q_rank = wq.shape[1:]
    rope = BLOCK // per
    half = rope // 2
    nope = head - rope
    quads = wq.shape[0] // 4
    duos = seqs // 2
    wide = 2 * BLOCK
    factor = LOG2E * head**-0.5

    loads = {}

    def load(name, src, dst):
        loads[name] = pltpu.make_async_copy(src, dst, load_sem.at[len(loads)])
        loads[name].start()

    def spot(slot, parity):
        return pl.ds(pl.multiple_of(prefix + slot * BLOCK + parity * toks, toks), toks)

    load("x0", x_hbm.at[pl.ds(0, per)], x_buf.at[pl.ds(0, per)])
    load("wdkv", wdkv_hbm, wdkv)
    load("wk", wk_hbm, wkv.at[pl.ds(0, heads), pl.ds(0, nope)])
    load("wv", wv_hbm, wkv.at[pl.ds(0, heads), pl.ds(nope, nope)])
    for g in range(1, groups):
        load(f"x{g}", x_hbm.at[pl.ds(g * per, per)], x_buf.at[pl.ds(g * per, per)])
    load("wdq", wdq_hbm, wdq)
    load("wq", wq_hbm, wq.at[pl.ds(0, heads)])
    load("pe", pe_hbm.at[:, :, pl.ds(0, prefix)], pe_buf)
    load("lat", lat_hbm.at[:, pl.ds(0, prefix)], rows.at[:, pl.ds(0, prefix)])

    barrier = pltpu.get_barrier_semaphore()
    for peer in (left, right, other):
        pl.semaphore_signal(barrier, inc=1, device_id={"tp": peer}, device_id_type=MESH)
    if paired:
        pl.semaphore_signal(barrier, inc=1, device_id={"dp": partner}, device_id_type=MESH)
    pl.semaphore_wait(barrier, 4 if paired else 3)

    wire = Wire(send_sem, recv_sem)

    def chain(name, here, there, places):
        near_left, near_right, opposite = places
        handed = jnp.where(odd == 0, near_left, near_right)
        wire.add(name + "R", lambda: here(0), lambda: there(near_left), tp=right)
        wire.add(name + "L", lambda: here(0), lambda: there(near_right), tp=left)
        wire.add(name + "O", lambda: there(handed), lambda: there(opposite), tp=onward)

    for g in range(groups):
        for name, ref in (("c", lambda slot, g=g: rows.at[pl.ds(g * per, per), spot(slot, odd)]), ("p", lambda slot, g=g: rot.at[g, spot(slot, odd)])):
            name = f"{name}{g}"
            chain(name, ref, ref, (1, 3, 2))
            for slot in range(slots):
                wire.add(f"{name}S{slot}", functools.partial(ref, slot), functools.partial(ref, slot), tp=other)
        cq_ref = lambda g=g: cq_buf.at[odd, pl.ds(g * per, per)]
        wire.add(f"q{g}S", cq_ref, cq_ref, tp=other)

    def cut(total, side, unit, part):
        if part == "mid":
            return pl.ds(side, total - 2 * side)
        flip = e if part == "mine" else 1 - e
        return pl.ds(pl.multiple_of(flip * (total - side), unit), side)

    def wq_at(part, slot):
        return wq.at[pl.ds(slot * heads, heads), :, cut(q_rank, q_rank // 3, BLOCK, part)]

    def wkv_at(part, slot):
        return wkv.at[pl.ds(slot * heads, heads), cut(2 * nope, 48, 16, part)]

    def wo_at(part, slot):
        return wo_out.at[odd, slot, cut(wo_hbm.shape[0], 80, 16, part)]

    def wo_own(part, slot):
        return wo_hbm.at[cut(wo_hbm.shape[0], 80, 16, part)]

    by_ring = ("mine", "mid") if paired else ("mine", "mid", "rest")
    for name, here, there in (("wq", wq_at, wq_at), ("wkv", wkv_at, wkv_at), ("wo", wo_own, wo_at)):
        for part in by_ring:
            chain(f"{name}.{part}", functools.partial(here, part), functools.partial(there, part), (1, 2, 3))
        if paired:
            for slot in (1, 2, 3):
                ref = functools.partial(there, "mine", slot)
                wire.add(f"{name}Z{slot}", ref, ref, dp=partner)
    late = ("mid",) if paired else ("mid", "rest")
    for slot in range(slots):
        mine = lambda slot=slot: wo_out.at[odd, slot]
        wire.add(f"woS{slot}", mine if slot else lambda: wo_hbm, mine, tp=other)
    for quad in range(quads):
        wire.add(f"o{quad}S", lambda quad=quad: o_send.at[quad], lambda quad=quad: o_out.at[1, quad], tp=other)

    def both(name, parts):
        return [f"{name}.{part}{way}" for part in parts for way in "RL"]

    def onwards(name, parts):
        return [f"{name}.{part}O" for part in parts]

    def across(name, *which):
        return [f"{name}Z{slot}" for slot in which] if paired else []

    loads["wk"].wait()
    loads["wv"].wait()
    wire.start(*both("wkv", ("mine",)))
    loads["wdkv"].wait()
    for g in range(groups):
        loads[f"x{g}"].wait()
    for g in range(groups):
        x = x_buf[g * per : (g + 1) * per].reshape(per * toks, dim).astype(F32)
        a = (unit(x) * g1_ref[...]).astype(BF16)
        a_buf[g] = a
        kv = dot_t(a, wdkv[...])
        rows[g * per : (g + 1) * per, spot(0, odd), :] = (unit(kv[:, :rank]) * gkv_ref[...]).astype(BF16).reshape(per, toks, rank)
        turned = []
        for s in range(per):
            lanes = pl.ds(pl.multiple_of(chip * BLOCK, BLOCK), BLOCK)
            cos_pair, sin_pair = cos_ref[g * per + s, :, lanes], sin_ref[g * per + s, :, lanes]
            cos = jnp.where(odd == 1, cos_pair[:, toks:], cos_pair[:, :toks])
            sin = jnp.where(odd == 1, sin_pair[:, toks:], sin_pair[:, :toks])
            table = jnp.concatenate([cos, cos, -sin, sin], axis=0).T
            p = kv[s * toks : (s + 1) * toks, rank:]
            swapped = jnp.concatenate([p[:, half:], p[:, :half]], axis=1)
            turned.append(p * table[:, :rope] + swapped * table[:, rope:])
        rot[g, spot(0, odd), :] = jnp.concatenate(turned, axis=1).astype(BF16)
        for way in ("R", "L", "S0"):
            wire.start(f"c{g}{way}", f"p{g}{way}")

    loads["wdq"].wait()
    for g in range(groups):
        h = dot(a_buf[g], wdq[...])
        cq_buf[odd, g * per : (g + 1) * per] = (unit(h) * gq_ref[...]).astype(BF16).reshape(per, toks, q_rank)
        wire.start(f"q{g}S")

    loads["pe"].wait()
    for g in range(groups):
        old = pe_buf[g * per : (g + 1) * per].reshape(per * rope, prefix).astype(F32)
        for b in range(prefix // BLOCK):
            rot[g, b * BLOCK : (b + 1) * BLOCK] = old[:, b * BLOCK : (b + 1) * BLOCK].T.astype(BF16)
    qb[...] = jnp.zeros_like(qb)

    for g in range(groups):
        wire.landed(f"c{g}R", f"p{g}R", f"c{g}L", f"p{g}L")
        wire.start(f"c{g}O", f"p{g}O", f"c{g}S1", f"p{g}S1", f"c{g}S3", f"p{g}S3")
    loads["wq"].wait()
    wire.start(*both("wq", ("mine",)), *both("wkv", late), *both("wq", late))
    wire.landed(*both("wkv", ("mine",)))
    wire.start(*across("wkv", 1, 2), *onwards("wkv", ("mine",)))

    def rest_of(g):
        wire.landed(f"c{g}O", f"p{g}O")
        wire.start(f"c{g}S2", f"p{g}S2")
        for slot in (0, 1, 3, 2):
            wire.landed(f"c{g}S{slot}", f"p{g}S{slot}")
        wire.landed(f"q{g}S")

    loads["lat"].wait()
    rest_of(0)

    row = lax.broadcasted_iota(jnp.int32, (BLOCK, wide), 0)
    lane = lax.rem(lax.broadcasted_iota(jnp.int32, (BLOCK, wide), 1), BLOCK)
    near = row <= lane
    lanes_chip = pl.ds(pl.multiple_of(chip * BLOCK, BLOCK), BLOCK)

    def place(n):
        return n // duos, lax.rem(n, duos)

    def query_stage(n):
        quad, duo = place(n)
        w = wq[pl.ds(quad * 4, 4)].reshape(4 * head, q_rank)
        cq = jnp.concatenate([cq_buf[parity, 2 * duo + u] for u in range(2) for parity in range(2)], axis=0)
        raw = dot_t(w, cq)
        for u in range(2):
            slot = 2 * lax.rem(duo, 2) + u
            cos, sin = cos_ref[2 * duo + u, :, lanes_chip], sin_ref[2 * duo + u, :, lanes_chip]
            for h in range(4):
                pair, side = h // 2, h % 2
                q = raw[h * head : (h + 1) * head, u * BLOCK : (u + 1) * BLOCK]
                cols = slice(side * BLOCK, (side + 1) * BLOCK)
                qb[u, pair, side * nope : (side + 1) * nope, cols] = q[:nope].astype(BF16)
                lo, hi = q[nope : nope + half], q[nope + half :]
                turned = jnp.concatenate([lo * cos - hi * sin, hi * cos + lo * sin], axis=0).astype(BF16)
                start = pl.multiple_of(BLOCK + slot * rope, rope)
                stale = pl.multiple_of(BLOCK + lax.rem(slot + 2, 4) * rope, rope)
                qb[u, pair, pl.ds(start, rope), cols] = turned
                qb[u, pair, pl.ds(stale, rope), cols] = jnp.zeros_like(turned)

    def key_stage(n, t):
        quad, duo = place(n)
        w = wkv[pl.ds(quad * 4, 4), :nope].reshape(4 * nope, rank)
        for u in range(2):
            kb[u, :t] = dot_t(rows[2 * duo + u, :t], w).astype(BF16)

    def value_stage(n, t):
        quad, duo = place(n)
        w = wkv[pl.ds(quad * 4, 4), nope:].reshape(4 * nope, rank)
        for u in range(2):
            vb[u, :, :t] = dot_t(w, rows[2 * duo + u, :t]).astype(BF16)

    def score_stage(n, t, u, pair):
        _, duo = place(n)
        length = len_ref[2 * duo + u]
        keys = jnp.concatenate([kb[u, :t, pair * BLOCK : (pair + 1) * BLOCK], rot[duo // 2, :t]], axis=1)
        value = dot(keys, qb[u, pair])
        most = None
        for b in range(t // BLOCK):
            part = value[b * BLOCK : (b + 1) * BLOCK]
            if BLOCK <= b * BLOCK < prefix:
                part = jnp.where(row < length - b * BLOCK, part, NEVER)
            if b * BLOCK == prefix:
                part = jnp.where(near, part, NEVER)
            sb[2 * u + pair][b * BLOCK : (b + 1) * BLOCK] = part
            part = jnp.max(part.reshape(BLOCK // 8, 8, wide), axis=0)
            most = part if most is None else jnp.maximum(most, part)
        mb[2 * u + pair] = jnp.broadcast_to(jnp.max(most, axis=0, keepdims=True), (8, wide))

    def soft_stage(t, u, pair):
        i = 2 * u + pair
        most = mb[i, :1]
        total = None
        for b in range(t // BLOCK):
            x = jnp.exp2((sb[i][b * BLOCK : (b + 1) * BLOCK] - most) * factor)
            part = jnp.sum(x.reshape(BLOCK // 8, 8, wide), axis=0)
            total = part if total is None else total + part
            pb[i][b * BLOCK : (b + 1) * BLOCK] = x.astype(BF16)
        lb[i] = total

    def mix_stage(n, t, u, pair):
        quad, duo = place(n)
        i = 2 * u + pair
        inv = 1.0 / jnp.sum(lb[i], axis=0, keepdims=True)
        o = dot(vb[u, pair * BLOCK : (pair + 1) * BLOCK, :t], pb[i][:t]) * inv
        o = jnp.concatenate([o[:nope, :BLOCK], o[nope:, BLOCK:]], axis=0).T.astype(BF16)
        first, second = o[:toks], o[toks:]
        cols = slice(pair * BLOCK, (pair + 1) * BLOCK)
        o_own[quad, 2 * duo + u, :, cols] = jnp.where(odd == 1, second, first)
        o_send[quad, 2 * duo + u, :, cols] = jnp.where(odd == 1, first, second)

    units = [(u, pair) for u in range(2) for pair in range(2)]
    total = quads * duos

    def each_chip(fn):
        for c in range(slots):
            pl.when(chip == c)(lambda c=c: fn(prefix + (c + 1) * BLOCK))

    def body(b, t):
        before, ahead, later = jnp.maximum(b - 1, 0), jnp.minimum(b + 1, total - 1), jnp.minimum(b + 2, total - 1)
        for u, pair in units:
            mix_stage(before, t, u, pair)
        value_stage(b, t)
        for u, pair in units:
            soft_stage(t, u, pair)
            score_stage(ahead, t, u, pair)
        key_stage(later, t)
        query_stage(later)

    def at(b, when):
        return pl.when(b == when)

    def step(b, _):
        @at(b, 0)
        def _():
            rest_of(1)

        @at(b, 2)
        def _():
            rest_of(2)
            pltpu.make_async_copy(rows.at[:, pl.ds(prefix, chunk)], c_out, load_sem.at[0]).start()
            pltpu.make_async_copy(rot.at[:, pl.ds(prefix, chunk)], p_out, load_sem.at[1]).start()

        @at(b, 3)
        def _():
            wire.landed(*both("wq", ("mine",)))
            wire.start(*across("wq", 1, 2), *onwards("wq", ("mine",)))

        @at(b, duos - 2)
        def _():
            wire.landed(*both("wkv", late), *both("wq", late))
            wire.start(*onwards("wkv", late), *onwards("wq", late))
            wire.start(*both("wo", ("mine",)), "woS0")
            wire.landed(*across("wkv", 1, 2), *across("wq", 1, 2))

        @at(b, 9)
        def _():
            wire.landed(*onwards("wkv", by_ring), *onwards("wq", by_ring))
            wire.start(*across("wkv", 3), *across("wq", 3))

        @at(b, 15)
        def _():
            wire.landed(*both("wo", ("mine",)))
            wire.start(*across("wo", 1, 2), *onwards("wo", ("mine",)), *both("wo", late))
            wire.landed(*across("wkv", 3), *across("wq", 3))

        @at(b, 25)
        def _():
            wire.landed(*onwards("wo", ("mine",)))
            wire.start(*across("wo", 3))

        @at(b, 27)
        def _():
            wire.landed(*both("wo", late))
            wire.start(*onwards("wo", late))

        for quad in range(quads - 1):
            at(b, (quad + 1) * duos + 1)(functools.partial(wire.start, f"o{quad}S"))

        each_chip(functools.partial(body, b))
        return 0

    def lead_in(t):
        key_stage(0, t)
        query_stage(0)

    def second(t):
        for u, pair in units:
            score_stage(0, t, u, pair)
        key_stage(1, t)
        query_stage(1)

    each_chip(lead_in)
    each_chip(second)
    lax.fori_loop(0, total, step, 0)

    def last(t):
        for u, pair in units:
            mix_stage(total - 1, t, u, pair)

    each_chip(last)
    wire.start(f"o{quads - 1}S")
    pltpu.make_async_copy(o_own, o_out.at[0], load_sem.at[2]).start()
    pltpu.make_async_copy(wo_hbm, wo_out.at[odd, 0], load_sem.at[3]).start()

    wire.landed(*across("wo", 1, 2))
    wire.start("woS1", "woS2")
    wire.landed(*onwards("wo", late), *across("wo", 3))
    wire.start("woS3")
    for slot in range(slots):
        wire.landed(f"woS{slot}")
    for quad in range(quads):
        wire.landed(f"o{quad}S")
    wire.sent(*wire.index)
    pltpu.make_async_copy(rows.at[:, pl.ds(prefix, chunk)], c_out, load_sem.at[0]).wait()
    pltpu.make_async_copy(rot.at[:, pl.ds(prefix, chunk)], p_out, load_sem.at[1]).wait()
    pltpu.make_async_copy(o_own, o_out.at[0], load_sem.at[2]).wait()
    pltpu.make_async_copy(wo_hbm, wo_out.at[odd, 0], load_sem.at[3]).wait()


def cache_kernel(len_ref, c_ref, p_ref, lat_ref, pe_ref, lat_out, pe_out, fresh, fresh_pe):
    step = pl.program_id(0)
    chip = lax.axis_index("tp") // 2
    per, slots, _, toks, rank = c_ref.shape
    rope = pe_ref.shape[1]
    cache_len = lat_ref.shape[1]
    chunk = slots * 2 * toks
    words = rank // BLOCK
    tile_row = lax.broadcasted_iota(jnp.int32, (16, BLOCK), 0)

    def slot_of(j):
        return lax.rem(chip - j + slots, slots)

    def one_sequence(s, _):
        length = len_ref[step * per + s]
        for j in range(slots):
            piece = c_ref[s, slot_of(j)].reshape(2 * toks, rank).astype(F32)
            for w in range(words):
                fresh[w, BLOCK + j * 2 * toks : BLOCK + (j + 1) * 2 * toks] = piece[:, w * BLOCK : (w + 1) * BLOCK]
        lat_out[s] = lat_ref[s]
        base = (length // 16) * 16
        skew = length - base

        def tile(k, partial):
            at = pl.multiple_of(base + k * 16, 16)
            for w in range(words):
                moved = fresh[w, pl.ds(BLOCK - skew + k * 16, 16), :].astype(BF16)
                cols = slice(w * BLOCK, (w + 1) * BLOCK)
                if partial:
                    local = tile_row + k * 16 - skew
                    moved = jnp.where((local >= 0) & (local < chunk), moved.astype(F32), lat_ref[s, pl.ds(at, 16), cols].astype(F32)).astype(BF16)
                lat_out[s, pl.ds(at, 16), cols] = moved

        for k in range(chunk // 16):
            tile(k, k == 0)
        pl.when(skew > 0)(functools.partial(tile, chunk // 16, True))
        return 0

    lax.fori_loop(0, per, one_sequence, 0)

    for j in range(slots):
        fresh_pe[cache_len - chunk + j * 2 * toks : cache_len - chunk + (j + 1) * 2 * toks] = p_ref[0, slot_of(j)].reshape(2 * toks, BLOCK).astype(F32)
    old = pe_ref[...].reshape(per * rope, cache_len).astype(F32)
    lane_seq = lax.broadcasted_iota(jnp.int32, (BLOCK, BLOCK), 1) // rope
    row = lax.broadcasted_iota(jnp.int32, (BLOCK, BLOCK), 0)
    for b in range(cache_len // BLOCK):
        value = old[:, b * BLOCK : (b + 1) * BLOCK].T
        for s in range(per):
            length = len_ref[step * per + s]
            moved = fresh_pe[pl.ds(b * BLOCK + cache_len - chunk - length, BLOCK), :]
            local = row + (b * BLOCK - length)
            value = jnp.where((lane_seq == s) & (local >= 0) & (local < chunk), moved, value)
        pe_out[:, :, b * BLOCK : (b + 1) * BLOCK] = value.T.astype(BF16).reshape(per, rope, BLOCK)


def output_kernel(o_ref, w_ref, x_ref, y_ref):
    odd = lax.rem(lax.axis_index("tp"), 2)
    _, quads, seqs, toks, depth = o_ref.shape
    slots, rows, wide = w_ref.shape[1:]
    y = x_ref[...].reshape(seqs * toks, wide).astype(F32)
    for side in range(2):
        w = w_ref[odd if side == 0 else 1 - odd].reshape(slots * rows, wide)
        for quad in range(quads):
            y = y + dot(o_ref[side, quad].reshape(seqs * toks, depth), w[quad * depth : (quad + 1) * depth])
    y_ref[...] = y.astype(BF16).reshape(y_ref.shape)


def solution(mesh):
    size = mesh.shape["tp"]
    paired = mesh.shape["dp"] % 2 == 0

    def local_step(hidden, lengths, rope_cos, rope_sin, cache_lat, cache_pe, norm_in, w_dq, norm_q, w_dkv, norm_kv, w_uq, w_uk, w_uv, w_out):
        seqs, toks, dim = hidden.shape
        q_rank = w_dq.shape[1]
        rank, heads, nope = w_uk.shape
        rope = cache_pe.shape[2]
        cache_len = cache_lat.shape[1]
        slots = size // 2
        head = nope + rope
        quads = slots * heads // 4
        chunk = size * toks
        prefix = cache_len - chunk
        per = BLOCK // rope
        groups = seqs // per
        wide = 2 * BLOCK
        cos_t, sin_t = rope_cos.transpose(0, 2, 1), rope_sin.transpose(0, 2, 1)
        pe_t = cache_pe.transpose(0, 2, 1)
        wdkv_t = w_dkv.transpose(1, 0)
        wq_t, wk_t, wv_t = (w.transpose(1, 2, 0) for w in (w_uq, w_uk, w_uv))

        any_spec = pl.BlockSpec(memory_space=pl.ANY)
        vmem_spec = pl.BlockSpec(memory_space=pltpu.VMEM)
        smem_spec = pl.BlockSpec(memory_space=pltpu.SMEM)
        c_all, p_all, o_all, wo_all = pl.pallas_call(
            functools.partial(main_kernel, (size, paired)),
            in_specs=[smem_spec, any_spec, vmem_spec, any_spec, vmem_spec, any_spec, vmem_spec, vmem_spec, vmem_spec] + [any_spec] * 6,
            out_specs=[any_spec] * 4,
            out_shape=[
                jax.ShapeDtypeStruct((seqs, chunk, rank), BF16),
                jax.ShapeDtypeStruct((groups, chunk, BLOCK), BF16),
                jax.ShapeDtypeStruct((2, quads, seqs, toks, 4 * nope), BF16),
                jax.ShapeDtypeStruct((2, slots) + w_out.shape, BF16),
            ],
            scratch_shapes=[
                pltpu.VMEM(hidden.shape, BF16),
                pltpu.VMEM(w_dq.shape, BF16),
                pltpu.VMEM(wdkv_t.shape, BF16),
                pltpu.VMEM((groups, per * toks, dim), BF16),
                pltpu.VMEM((seqs, cache_len, rank), BF16),
                pltpu.VMEM((groups, cache_len, BLOCK), BF16),
                pltpu.VMEM((seqs, rope, prefix), BF16),
                pltpu.VMEM((2, seqs, toks, q_rank), BF16),
                pltpu.VMEM((slots * heads, head, q_rank), BF16),
                pltpu.VMEM((slots * heads, 2 * nope, rank), BF16),
                pltpu.VMEM((2, cache_len, 4 * nope), BF16),
                pltpu.VMEM((2, 4 * nope, cache_len), BF16),
                pltpu.VMEM((2, 2, wide, wide), BF16),
                [pltpu.VMEM((cache_len, wide), F32) for _ in range(4)],
                pltpu.VMEM((4, 8, wide), F32),
                [pltpu.VMEM((cache_len, wide), BF16) for _ in range(4)],
                pltpu.VMEM((4, 8, wide), F32),
                pltpu.VMEM((quads, seqs, toks, 4 * nope), BF16),
                pltpu.VMEM((quads, seqs, toks, 4 * nope), BF16),
                pltpu.SemaphoreType.DMA((8 + groups,)),
                pltpu.SemaphoreType.DMA((128,)),
                pltpu.SemaphoreType.DMA((128,)),
            ],
            compiler_params=pltpu.CompilerParams(collective_id=0, has_side_effects=True, vmem_limit_bytes=63 * MIB),
            cost_estimate=pl.CostEstimate(flops=70 * 10**9, bytes_accessed=40 * MIB, transcendentals=30 * 10**6),
            name="main",
        )(lengths, hidden, norm_in, w_dq, norm_q, wdkv_t, norm_kv, cos_t, sin_t, wq_t, wk_t, wv_t, w_out, cache_lat, pe_t)

        c_all = c_all.reshape(seqs, slots, 2, toks, rank)
        p_all = p_all.reshape(groups, slots, 2, toks, BLOCK)
        lat_new, pe_new = pl.pallas_call(
            cache_kernel,
            grid_spec=pltpu.PrefetchScalarGridSpec(
                num_scalar_prefetch=1,
                grid=(groups,),
                in_specs=[
                    pl.BlockSpec((per, slots, 2, toks, rank), lambda i, n: (i, 0, 0, 0, 0)),
                    pl.BlockSpec((1, slots, 2, toks, BLOCK), lambda i, n: (i, 0, 0, 0, 0)),
                    pl.BlockSpec((per, cache_len, rank), lambda i, n: (i, 0, 0)),
                    pl.BlockSpec((per, rope, cache_len), lambda i, n: (i, 0, 0)),
                ],
                out_specs=[
                    pl.BlockSpec((per, cache_len, rank), lambda i, n: (i, 0, 0)),
                    pl.BlockSpec((per, rope, cache_len), lambda i, n: (i, 0, 0)),
                ],
                scratch_shapes=[
                    pltpu.VMEM((rank // BLOCK, chunk + 2 * BLOCK, BLOCK), F32),
                    pltpu.VMEM((2 * cache_len - chunk, BLOCK), F32),
                ],
            ),
            out_shape=[jax.ShapeDtypeStruct(cache_lat.shape, BF16), jax.ShapeDtypeStruct(pe_t.shape, BF16)],
            compiler_params=pltpu.CompilerParams(vmem_limit_bytes=63 * MIB),
            cost_estimate=pl.CostEstimate(flops=4 * 10**9, bytes_accessed=20 * MIB, transcendentals=0),
            name="cache",
        )(lengths, c_all, p_all, cache_lat, pe_t)

        part = 512
        y = pl.pallas_call(
            output_kernel,
            grid=(dim // part,),
            in_specs=[
                pl.BlockSpec(o_all.shape, lambda i: (0, 0, 0, 0, 0), pipeline_mode=pl.Buffered(1)),
                pl.BlockSpec(wo_all.shape[:3] + (part,), lambda i: (0, 0, 0, i)),
                pl.BlockSpec((seqs, toks, part), lambda i: (0, 0, i)),
            ],
            out_specs=pl.BlockSpec((seqs, toks, part), lambda i: (0, 0, i)),
            out_shape=jax.ShapeDtypeStruct(hidden.shape, BF16),
            compiler_params=pltpu.CompilerParams(vmem_limit_bytes=63 * MIB),
            cost_estimate=pl.CostEstimate(flops=2 * seqs * toks * dim * dim, bytes_accessed=30 * MIB, transcendentals=0),
            name="output",
        )(o_all, wo_all, hidden)
        return y, lat_new, pe_new.transpose(0, 2, 1)

    spec_tok = P("dp", "tp", None)
    spec_len = P("dp")
    spec_seq = P("dp", None, None)
    spec_vec = P(None)
    spec_mat = P(None, None)
    spec_head = P(None, "tp", None)
    spec_rows = P("tp", None)
    in_specs = (spec_tok, spec_len, spec_seq, spec_seq, spec_seq, spec_seq, spec_vec, spec_mat, spec_vec, spec_mat, spec_vec, spec_head, spec_head, spec_head, spec_rows)
    return jax.shard_map(local_step, mesh=mesh, in_specs=in_specs, out_specs=(spec_tok, spec_seq, spec_seq), check_vma=False)
```

time: 1030 us -> 181 us (0.18)
  the two profiles are of different devices: /device:TPU:81 before, /device:TPU:87 now
where the time goes in v3:
time: 181 us
  Pallas kernels  180 us (99%)
    pallas_call x1, Pallas kernels, local_step(): pl.pallas_call(functools.partial(main_kernel, (size, paired)), in_specs=[...  154 us
    pallas_call x1, Pallas kernels, local_step(): pl.pallas_call(output_kernel, grid=(dim // part,), in_specs=[pl.BlockSpec...  15.2 us
    pallas_call x1, Pallas kernels, local_step(): pl.pallas_call(cache_kernel, grid_spec=pltpu.PrefetchScalarGridSpec(num_s...  10.4 us

profile of v3, /device:TPU:87, one launch (start us, length us, event | category | flops | bytes accessed | tf_op | source)
XLA Modules:
  0.0 180.7 jit_solution(15618391424254695508)
XLA Ops:
  0.6 154.5 %main.1 = (bf16[12,512,256]{2,1,0:T(8,128)(2,1)}, bf16[3,512,128]{2,1,0:T(8,128)(2,1)}, bf16[2,5,12,64,256]{4,3,2,1,0:T(8,128)(2,1)}, bf16[2,4,320,2560]{3,2,1,0:T(8,128)(2,1)}) custom-call(s32[12]{0:T(128)} %len_ref.3, bf16[12,64,2560]{2,1,0:T(8,128)(2,1)} %x_ref.1, f32[2560]{0:T(1024)} %g1_ref.1, bf16[2560,768]{1,0:T(8,128)(2,1)} %wdq_hbm.1, f32[768]{0:T(1024)} %gq_ref.1, ...), custom_call_target="tpu_custom_call" | custom-call | flops 70000001024 | bytes 41943040 | tf_op jit(solution)/shard_map/main/pallas_call | solution.py:553
  155.1 15.2 %output.1 = bf16[12,64,2560]{2,1,0:T(8,128)(2,1)} custom-call(bf16[2,5,12,64,256]{4,3,2,1,0:T(8,128)(2,1)} %get-tuple-element.9.o_ref, bf16[2,4,320,2560]{3,2,1,0:T(8,128)(2,1)} %get-tuple-element.10.w_ref, bf16[12,64,2560]{2,1,0:T(8,128)(2,1)} %x_ref.1), custom_call_target="tpu_custom_call" | custom-call | flops 10066329600 | bytes 31457280 | tf_op jit(solution)/shard_map/output/pallas_call | solution.py:621
  170.3 10.4 %cache.1 = (bf16[12,1024,256]{2,1,0:T(8,128)(2,1)}, bf16[12,32,1024]{2,1,0:T(8,128)(2,1)}) custom-call(s32[12]{0:T(128)} %len_ref.3, bf16[12,4,2,64,256]{4,3,2,1,0:T(8,128)(2,1)} %bitcast.18, bf16[3,4,2,64,128]{4,3,2,1,0:T(8,128)(2,1)} %bitcast.20, bf16[12,1024,256]{2,1,0:T(8,128)(2,1)} %lat_ref.1, bf16[12,32,1024]{2,1,0:T(8,128)(2,1)} %bitcast.12), custom_call_target="tpu_custom_call" | custom-call | flops 4000000000 | bytes 20971520 | tf_op jit(solution)/shard_map/cache/pallas_call | solution.py:594

commit v4 on v3

--- a/solution.py
+++ b/solution.py
@@ -62,8 +62,8 @@
     gq_ref,
     wdkv_hbm,
     gkv_ref,
-    cos_ref,
-    sin_ref,
+    cos_hbm,
+    sin_hbm,
     wq_hbm,
     wk_hbm,
     wv_hbm,
@@ -81,12 +81,15 @@
     rows,
     rot,
     pe_buf,
+    cos_ref,
+    sin_ref,
     cq_buf,
     wq,
     wkv,
     kb,
     vb,
     qb,
+    q_raw,
     sb,
     mb,
     pb,
@@ -134,37 +137,40 @@
     def spot(slot, parity):
         return pl.ds(pl.multiple_of(prefix + slot * BLOCK + parity * toks, toks), toks)
 
-    load("x0", x_hbm.at[pl.ds(0, per)], x_buf.at[pl.ds(0, per)])
-    load("wdkv", wdkv_hbm, wdkv)
-    load("wk", wk_hbm, wkv.at[pl.ds(0, heads), pl.ds(0, nope)])
-    load("wv", wv_hbm, wkv.at[pl.ds(0, heads), pl.ds(nope, nope)])
-    for g in range(1, groups):
-        load(f"x{g}", x_hbm.at[pl.ds(g * per, per)], x_buf.at[pl.ds(g * per, per)])
-    load("wdq", wdq_hbm, wdq)
-    load("wq", wq_hbm, wq.at[pl.ds(0, heads)])
-    load("pe", pe_hbm.at[:, :, pl.ds(0, prefix)], pe_buf)
-    load("lat", lat_hbm.at[:, pl.ds(0, prefix)], rows.at[:, pl.ds(0, prefix)])
-
     barrier = pltpu.get_barrier_semaphore()
     for peer in (left, right, other):
         pl.semaphore_signal(barrier, inc=1, device_id={"tp": peer}, device_id_type=MESH)
     if paired:
         pl.semaphore_signal(barrier, inc=1, device_id={"dp": partner}, device_id_type=MESH)
+
+    lanes_chip = pl.ds(pl.multiple_of(chip * BLOCK, BLOCK), BLOCK)
+    load("wk", wk_hbm, wkv.at[pl.ds(0, heads), pl.ds(0, nope)])
+    load("wv", wv_hbm, wkv.at[pl.ds(0, heads), pl.ds(nope, nope)])
+    for g in range(groups):
+        load(f"x{g}", x_hbm.at[pl.ds(g * per, per)], x_buf.at[pl.ds(g * per, per)])
+        if g == 0:
+            load("wdkv", wdkv_hbm, wdkv)
+            load("cos", cos_hbm.at[:, :, lanes_chip], cos_ref)
+            load("sin", sin_hbm.at[:, :, lanes_chip], sin_ref)
+    load("wq", wq_hbm, wq.at[pl.ds(0, heads)])
+    load("wdq", wdq_hbm, wdq)
+    load("pe", pe_hbm.at[:, :, pl.ds(0, prefix)], pe_buf)
+    load("lat", lat_hbm.at[:, pl.ds(0, prefix)], rows.at[:, pl.ds(0, prefix)])
     pl.semaphore_wait(barrier, 4 if paired else 3)
 
     wire = Wire(send_sem, recv_sem)
 
-    def chain(name, here, there, places):
+    def chain(name, here, there, places, via="split"):
         near_left, near_right, opposite = places
-        handed = jnp.where(odd == 0, near_left, near_right)
+        handed = {"right": near_left, "left": near_right, "split": jnp.where(odd == 0, near_left, near_right)}[via]
         wire.add(name + "R", lambda: here(0), lambda: there(near_left), tp=right)
         wire.add(name + "L", lambda: here(0), lambda: there(near_right), tp=left)
-        wire.add(name + "O", lambda: there(handed), lambda: there(opposite), tp=onward)
+        wire.add(name + "O", lambda: there(handed), lambda: there(opposite), tp={"right": right, "left": left, "split": onward}[via])
 
     for g in range(groups):
         for name, ref in (("c", lambda slot, g=g: rows.at[pl.ds(g * per, per), spot(slot, odd)]), ("p", lambda slot, g=g: rot.at[g, spot(slot, odd)])):
             name = f"{name}{g}"
-            chain(name, ref, ref, (1, 3, 2))
+            chain(name, ref, ref, (1, 3, 2), "left")
             for slot in range(slots):
                 wire.add(f"{name}S{slot}", functools.partial(ref, slot), functools.partial(ref, slot), tp=other)
         cq_ref = lambda g=g: cq_buf.at[odd, pl.ds(g * per, per)]
@@ -191,7 +197,7 @@
     by_ring = ("mine", "mid") if paired else ("mine", "mid", "rest")
     for name, here, there in (("wq", wq_at, wq_at), ("wkv", wkv_at, wkv_at), ("wo", wo_own, wo_at)):
         for part in by_ring:
-            chain(f"{name}.{part}", functools.partial(here, part), functools.partial(there, part), (1, 2, 3))
+            chain(f"{name}.{part}", functools.partial(here, part), functools.partial(there, part), (1, 2, 3), "right" if part == "mine" and name != "wo" else "split")
         if paired:
             for slot in (1, 2, 3):
                 ref = functools.partial(there, "mine", slot)
@@ -212,22 +218,20 @@
     def across(name, *which):
         return [f"{name}Z{slot}" for slot in which] if paired else []
 
-    loads["wk"].wait()
-    loads["wv"].wait()
-    wire.start(*both("wkv", ("mine",)))
-    loads["wdkv"].wait()
-    for g in range(groups):
-        loads[f"x{g}"].wait()
-    for g in range(groups):
-        x = x_buf[g * per : (g + 1) * per].reshape(per * toks, dim).astype(F32)
-        a = (unit(x) * g1_ref[...]).astype(BF16)
-        a_buf[g] = a
-        kv = dot_t(a, wdkv[...])
+    def ways(name, parts, which):
+        return [f"{name}.{part}{way}" for part in parts for way in which]
+
+    def norm(g):
+        for r in range(0, per):
+            x = x_buf[g * per + r].astype(F32)
+            a_buf[g, r * toks : (r + 1) * toks] = (unit(x) * g1_ref[...]).astype(BF16)
+
+    def latent(g):
+        kv = dot_t(a_buf[g], wdkv[...])
         rows[g * per : (g + 1) * per, spot(0, odd), :] = (unit(kv[:, :rank]) * gkv_ref[...]).astype(BF16).reshape(per, toks, rank)
         turned = []
         for s in range(per):
-            lanes = pl.ds(pl.multiple_of(chip * BLOCK, BLOCK), BLOCK)
-            cos_pair, sin_pair = cos_ref[g * per + s, :, lanes], sin_ref[g * per + s, :, lanes]
+            cos_pair, sin_pair = cos_ref[g * per + s], sin_ref[g * per + s]
             cos = jnp.where(odd == 1, cos_pair[:, toks:], cos_pair[:, :toks])
             sin = jnp.where(odd == 1, sin_pair[:, toks:], sin_pair[:, :toks])
             table = jnp.concatenate([cos, cos, -sin, sin], axis=0).T
@@ -235,13 +239,42 @@
             swapped = jnp.concatenate([p[:, half:], p[:, :half]], axis=1)
             turned.append(p * table[:, :rope] + swapped * table[:, rope:])
         rot[g, spot(0, odd), :] = jnp.concatenate(turned, axis=1).astype(BF16)
+
+    def queries(g):
+        h = jnp.concatenate([dot(a_buf[g], wdq[:, : 2 * rank]), dot(a_buf[g], wdq[:, 2 * rank :])], axis=1)
+        cq_buf[odd, g * per : (g + 1) * per] = (unit(h) * gq_ref[...]).astype(BF16).reshape(per, toks, q_rank)
+
+    loads["wk"].wait()
+    loads["wv"].wait()
+    wire.start(*both("wkv", ("mine",)))
+    for name in ("x0", "wdkv", "cos", "sin"):
+        loads[name].wait()
+    norm(0)
+    for g in range(groups):
+        if g + 1 < groups:
+            loads[f"x{g + 1}"].wait()
+            norm(g + 1)
+        latent(g)
         for way in ("R", "L", "S0"):
             wire.start(f"c{g}{way}", f"p{g}{way}")
+    loads["wq"].wait()
+    wire.start(*ways("wq", ("mine",), "R"), *ways("wkv", late, "R"), *ways("wq", late, "R"))
+
+    def hand_on(g):
+        wire.landed(f"c{g}R", f"p{g}R", f"c{g}L", f"p{g}L")
+        wire.start(f"c{g}O", f"p{g}O", f"c{g}S1", f"p{g}S1", f"c{g}S3", f"p{g}S3")
 
     loads["wdq"].wait()
-    for g in range(groups):
-        h = dot(a_buf[g], wdq[...])
-        cq_buf[odd, g * per : (g + 1) * per] = (unit(h) * gq_ref[...]).astype(BF16).reshape(per, toks, q_rank)
+    queries(0)
+    wire.start("q0S")
+    hand_on(0)
+    queries(1)
+    wire.start("q1S")
+    hand_on(1)
+    wire.landed(*both("wkv", ("mine",)))
+    wire.start(*across("wkv", 1, 2), *onwards("wkv", ("mine",)))
+    for g in range(2, groups):
+        queries(g)
         wire.start(f"q{g}S")
 
     loads["pe"].wait()
@@ -251,13 +284,9 @@
             rot[g, b * BLOCK : (b + 1) * BLOCK] = old[:, b * BLOCK : (b + 1) * BLOCK].T.astype(BF16)
     qb[...] = jnp.zeros_like(qb)
 
-    for g in range(groups):
-        wire.landed(f"c{g}R", f"p{g}R", f"c{g}L", f"p{g}L")
-        wire.start(f"c{g}O", f"p{g}O", f"c{g}S1", f"p{g}S1", f"c{g}S3", f"p{g}S3")
-    loads["wq"].wait()
-    wire.start(*both("wq", ("mine",)), *both("wkv", late), *both("wq", late))
-    wire.landed(*both("wkv", ("mine",)))
-    wire.start(*across("wkv", 1, 2), *onwards("wkv", ("mine",)))
+    for g in range(2, groups):
+        hand_on(g)
+    wire.start(*ways("wq", ("mine",), "L"), *ways("wkv", late, "L"), *ways("wq", late, "L"), *ways("wo", ("mine",), "L"), "woS0")
 
     def rest_of(g):
         wire.landed(f"c{g}O", f"p{g}O")
@@ -272,19 +301,22 @@
     row = lax.broadcasted_iota(jnp.int32, (BLOCK, wide), 0)
     lane = lax.rem(lax.broadcasted_iota(jnp.int32, (BLOCK, wide), 1), BLOCK)
     near = row <= lane
-    lanes_chip = pl.ds(pl.multiple_of(chip * BLOCK, BLOCK), BLOCK)
 
     def place(n):
         return n // duos, lax.rem(n, duos)
 
-    def query_stage(n):
+    def query_dot(n):
         quad, duo = place(n)
         w = wq[pl.ds(quad * 4, 4)].reshape(4 * head, q_rank)
         cq = jnp.concatenate([cq_buf[parity, 2 * duo + u] for u in range(2) for parity in range(2)], axis=0)
-        raw = dot_t(w, cq)
+        q_raw[...] = dot_t(w, cq)
+
+    def query_stage(n):
+        quad, duo = place(n)
+        raw = q_raw
         for u in range(2):
             slot = 2 * lax.rem(duo, 2) + u
-            cos, sin = cos_ref[2 * duo + u, :, lanes_chip], sin_ref[2 * duo + u, :, lanes_chip]
+            cos, sin = cos_ref[2 * duo + u], sin_ref[2 * duo + u]
             for h in range(4):
                 pair, side = h // 2, h % 2
                 q = raw[h * head : (h + 1) * head, u * BLOCK : (u + 1) * BLOCK]
@@ -297,22 +329,20 @@
                 qb[u, pair, pl.ds(start, rope), cols] = turned
                 qb[u, pair, pl.ds(stale, rope), cols] = jnp.zeros_like(turned)
 
-    def key_stage(n, t):
+    def key_stage(n, t, u):
         quad, duo = place(n)
         w = wkv[pl.ds(quad * 4, 4), :nope].reshape(4 * nope, rank)
-        for u in range(2):
-            kb[u, :t] = dot_t(rows[2 * duo + u, :t], w).astype(BF16)
-
-    def value_stage(n, t):
+        kb[u][:t] = dot_t(rows[2 * duo + u, :t], w).astype(BF16)
+
+    def value_stage(n, t, u):
         quad, duo = place(n)
         w = wkv[pl.ds(quad * 4, 4), nope:].reshape(4 * nope, rank)
-        for u in range(2):
-            vb[u, :, :t] = dot_t(w, rows[2 * duo + u, :t]).astype(BF16)
+        vb[u][:, :t] = dot_t(w, rows[2 * duo + u, :t]).astype(BF16)
 
     def score_stage(n, t, u, pair):
         _, duo = place(n)
         length = len_ref[2 * duo + u]
-        keys = jnp.concatenate([kb[u, :t, pair * BLOCK : (pair + 1) * BLOCK], rot[duo // 2, :t]], axis=1)
+        keys = jnp.concatenate([kb[u][:t, pair * BLOCK : (pair + 1) * BLOCK], rot[duo // 2, :t]], axis=1)
         value = dot(keys, qb[u, pair])
         most = None
         for b in range(t // BLOCK):
@@ -341,7 +371,7 @@
         quad, duo = place(n)
         i = 2 * u + pair
         inv = 1.0 / jnp.sum(lb[i], axis=0, keepdims=True)
-        o = dot(vb[u, pair * BLOCK : (pair + 1) * BLOCK, :t], pb[i][:t]) * inv
+        o = dot(vb[u][pair * BLOCK : (pair + 1) * BLOCK, :t], pb[i][:t]) * inv
         o = jnp.concatenate([o[:nope, :BLOCK], o[nope:, BLOCK:]], axis=0).T.astype(BF16)
         first, second = o[:toks], o[toks:]
         cols = slice(pair * BLOCK, (pair + 1) * BLOCK)
@@ -357,13 +387,23 @@
 
     def body(b, t):
         before, ahead, later = jnp.maximum(b - 1, 0), jnp.minimum(b + 1, total - 1), jnp.minimum(b + 2, total - 1)
-        for u, pair in units:
-            mix_stage(before, t, u, pair)
-        value_stage(b, t)
-        for u, pair in units:
-            soft_stage(t, u, pair)
-            score_stage(ahead, t, u, pair)
-        key_stage(later, t)
+        mix_stage(before, t, 0, 0)
+        soft_stage(t, 0, 0)
+        score_stage(ahead, t, 0, 0)
+        mix_stage(before, t, 0, 1)
+        value_stage(b, t, 0)
+        soft_stage(t, 0, 1)
+        score_stage(ahead, t, 0, 1)
+        mix_stage(before, t, 1, 0)
+        mix_stage(before, t, 1, 1)
+        key_stage(later, t, 0)
+        soft_stage(t, 1, 0)
+        score_stage(ahead, t, 1, 0)
+        value_stage(b, t, 1)
+        soft_stage(t, 1, 1)
+        score_stage(ahead, t, 1, 1)
+        key_stage(later, t, 1)
+        query_dot(later)
         query_stage(later)
 
     def at(b, when):
@@ -380,35 +420,45 @@
             pltpu.make_async_copy(rows.at[:, pl.ds(prefix, chunk)], c_out, load_sem.at[0]).start()
             pltpu.make_async_copy(rot.at[:, pl.ds(prefix, chunk)], p_out, load_sem.at[1]).start()
 
-        @at(b, 3)
-        def _():
-            wire.landed(*both("wq", ("mine",)))
-            wire.start(*across("wq", 1, 2), *onwards("wq", ("mine",)))
+        @at(b, 1)
+        def _():
+            wire.landed(*ways("wq", ("mine",), "R"))
+            wire.start(*across("wq", 1), *onwards("wq", ("mine",)))
 
         @at(b, duos - 2)
         def _():
-            wire.landed(*both("wkv", late), *both("wq", late))
+            wire.landed(*ways("wkv", late, "R"), *ways("wq", late, "R"), *across("wkv", 1), *across("wq", 1))
+            wire.start(*ways("wo", ("mine",), "R"))
+
+        @at(b, duos - 1)
+        def _():
+            wire.landed(*ways("wq", ("mine",), "L"))
+            wire.start(*across("wq", 2))
+
+        @at(b, 9)
+        def _():
+            wire.landed(*ways("wkv", late, "L"), *ways("wq", late, "L"), *across("wkv", 2), *across("wq", 2))
             wire.start(*onwards("wkv", late), *onwards("wq", late))
-            wire.start(*both("wo", ("mine",)), "woS0")
-            wire.landed(*across("wkv", 1, 2), *across("wq", 1, 2))
-
-        @at(b, 9)
+
+        @at(b, 14)
         def _():
             wire.landed(*onwards("wkv", by_ring), *onwards("wq", by_ring))
             wire.start(*across("wkv", 3), *across("wq", 3))
-
-        @at(b, 15)
-        def _():
-            wire.landed(*both("wo", ("mine",)))
-            wire.start(*across("wo", 1, 2), *onwards("wo", ("mine",)), *both("wo", late))
+            wire.landed(*ways("wo", ("mine",), "L"))
+            wire.start(*across("wo", 2), *ways("wo", late, "L"))
+
+        @at(b, 16)
+        def _():
             wire.landed(*across("wkv", 3), *across("wq", 3))
-
-        @at(b, 25)
+            wire.landed(*ways("wo", ("mine",), "R"))
+            wire.start(*across("wo", 1), *onwards("wo", ("mine",)), *ways("wo", late, "R"))
+
+        @at(b, 22)
         def _():
             wire.landed(*onwards("wo", ("mine",)))
             wire.start(*across("wo", 3))
 
-        @at(b, 27)
+        @at(b, 28)
         def _():
             wire.landed(*both("wo", late))
             wire.start(*onwards("wo", late))
@@ -420,13 +470,17 @@
         return 0
 
     def lead_in(t):
-        key_stage(0, t)
+        for u in range(2):
+            key_stage(0, t, u)
+        query_dot(0)
         query_stage(0)
 
     def second(t):
         for u, pair in units:
             score_stage(0, t, u, pair)
-        key_stage(1, t)
+        for u in range(2):
+            key_stage(1, t, u)
+        query_dot(1)
         query_stage(1)
 
     each_chip(lead_in)
@@ -440,7 +494,6 @@
     each_chip(last)
     wire.start(f"o{quads - 1}S")
     pltpu.make_async_copy(o_own, o_out.at[0], load_sem.at[2]).start()
-    pltpu.make_async_copy(wo_hbm, wo_out.at[odd, 0], load_sem.at[3]).start()
 
     wire.landed(*across("wo", 1, 2))
     wire.start("woS1", "woS2")
@@ -454,7 +507,6 @@
     pltpu.make_async_copy(rows.at[:, pl.ds(prefix, chunk)], c_out, load_sem.at[0]).wait()
     pltpu.make_async_copy(rot.at[:, pl.ds(prefix, chunk)], p_out, load_sem.at[1]).wait()
     pltpu.make_async_copy(o_own, o_out.at[0], load_sem.at[2]).wait()
-    pltpu.make_async_copy(wo_hbm, wo_out.at[odd, 0], load_sem.at[3]).wait()
 
 
 def cache_kernel(len_ref, c_ref, p_ref, lat_ref, pe_ref, lat_out, pe_out, fresh, fresh_pe):
@@ -512,13 +564,16 @@
         pe_out[:, :, b * BLOCK : (b + 1) * BLOCK] = value.T.astype(BF16).reshape(per, rope, BLOCK)
 
 
-def output_kernel(o_ref, w_ref, x_ref, y_ref):
+def output_kernel(o_ref, own_ref, w_ref, x_ref, y_ref):
     odd = lax.rem(lax.axis_index("tp"), 2)
     _, quads, seqs, toks, depth = o_ref.shape
     slots, rows, wide = w_ref.shape[1:]
     y = x_ref[...].reshape(seqs * toks, wide).astype(F32)
     for side in range(2):
-        w = w_ref[odd if side == 0 else 1 - odd].reshape(slots * rows, wide)
+        parity = odd if side == 0 else 1 - odd
+        w = w_ref[parity].reshape(slots * rows, wide)
+        if side == 0:
+            w = jnp.concatenate([own_ref[...], w[rows:]], axis=0)
         for quad in range(quads):
             y = y + dot(o_ref[side, quad].reshape(seqs * toks, depth), w[quad * depth : (quad + 1) * depth])
     y_ref[...] = y.astype(BF16).reshape(y_ref.shape)
@@ -552,7 +607,7 @@
         smem_spec = pl.BlockSpec(memory_space=pltpu.SMEM)
         c_all, p_all, o_all, wo_all = pl.pallas_call(
             functools.partial(main_kernel, (size, paired)),
-            in_specs=[smem_spec, any_spec, vmem_spec, any_spec, vmem_spec, any_spec, vmem_spec, vmem_spec, vmem_spec] + [any_spec] * 6,
+            in_specs=[smem_spec, any_spec, vmem_spec, any_spec, vmem_spec, any_spec, vmem_spec] + [any_spec] * 8,
             out_specs=[any_spec] * 4,
             out_shape=[
                 jax.ShapeDtypeStruct((seqs, chunk, rank), BF16),
@@ -568,19 +623,22 @@
                 pltpu.VMEM((seqs, cache_len, rank), BF16),
                 pltpu.VMEM((groups, cache_len, BLOCK), BF16),
                 pltpu.VMEM((seqs, rope, prefix), BF16),
+                pltpu.VMEM((seqs, rope // 2, BLOCK), F32),
+                pltpu.VMEM((seqs, rope // 2, BLOCK), F32),
                 pltpu.VMEM((2, seqs, toks, q_rank), BF16),
                 pltpu.VMEM((slots * heads, head, q_rank), BF16),
                 pltpu.VMEM((slots * heads, 2 * nope, rank), BF16),
-                pltpu.VMEM((2, cache_len, 4 * nope), BF16),
-                pltpu.VMEM((2, 4 * nope, cache_len), BF16),
+                [pltpu.VMEM((cache_len, 4 * nope), BF16) for _ in range(2)],
+                [pltpu.VMEM((4 * nope, cache_len), BF16) for _ in range(2)],
                 pltpu.VMEM((2, 2, wide, wide), BF16),
+                pltpu.VMEM((4 * head, wide), F32),
                 [pltpu.VMEM((cache_len, wide), F32) for _ in range(4)],
                 pltpu.VMEM((4, 8, wide), F32),
                 [pltpu.VMEM((cache_len, wide), BF16) for _ in range(4)],
                 pltpu.VMEM((4, 8, wide), F32),
                 pltpu.VMEM((quads, seqs, toks, 4 * nope), BF16),
                 pltpu.VMEM((quads, seqs, toks, 4 * nope), BF16),
-                pltpu.SemaphoreType.DMA((8 + groups,)),
+                pltpu.SemaphoreType.DMA((10 + groups,)),
                 pltpu.SemaphoreType.DMA((128,)),
                 pltpu.SemaphoreType.DMA((128,)),
             ],
@@ -623,6 +681,7 @@
             grid=(dim // part,),
             in_specs=[
                 pl.BlockSpec(o_all.shape, lambda i: (0, 0, 0, 0, 0), pipeline_mode=pl.Buffered(1)),
+                pl.BlockSpec((w_out.shape[0], part), lambda i: (0, i)),
                 pl.BlockSpec(wo_all.shape[:3] + (part,), lambda i: (0, 0, 0, i)),
                 pl.BlockSpec((seqs, toks, part), lambda i: (0, 0, i)),
             ],
@@ -631,7 +690,7 @@
             compiler_params=pltpu.CompilerParams(vmem_limit_bytes=63 * MIB),
             cost_estimate=pl.CostEstimate(flops=2 * seqs * toks * dim * dim, bytes_accessed=30 * MIB, transcendentals=0),
             name="output",
-        )(o_all, wo_all, hidden)
+        )(o_all, w_out, wo_all, hidden)
         return y, lat_new, pe_new.transpose(0, 2, 1)
 
     spec_tok = P("dp", "tp", None)

time: 181 us -> 134 us (0.74)
  the two profiles are of different devices: /device:TPU:87 before, /device:TPU:81 now
where the time goes in v4:
time: 134 us
  Pallas kernels  134 us (100%)
    pallas_call x1, Pallas kernels, local_step(): pl.pallas_call(functools.partial(main_kernel, (size, paired)), in_specs=[...  107 us
    pallas_call x1, Pallas kernels, local_step(): pl.pallas_call(output_kernel, grid=(dim // part,), in_specs=[pl.BlockSpec...  16.2 us
    pallas_call x1, Pallas kernels, local_step(): pl.pallas_call(cache_kernel, grid_spec=pltpu.PrefetchScalarGridSpec(num_s...  10.4 us

profile of v4, /device:TPU:81, one launch (start us, length us, event | category | flops | bytes accessed | tf_op | source)
XLA Modules:
  0.0 134.2 jit_solution(14193566002009301559)
XLA Ops:
  0.6 106.9 %main.1 = (bf16[12,512,256]{2,1,0:T(8,128)(2,1)}, bf16[3,512,128]{2,1,0:T(8,128)(2,1)}, bf16[2,5,12,64,256]{4,3,2,1,0:T(8,128)(2,1)}, bf16[2,4,320,2560]{3,2,1,0:T(8,128)(2,1)}) custom-call(s32[12]{0:T(128)} %len_ref.3, bf16[12,64,2560]{2,1,0:T(8,128)(2,1)} %x_ref.1, f32[2560]{0:T(1024)} %g1_ref.1, bf16[2560,768]{1,0:T(8,128)(2,1)} %wdq_hbm.1, f32[768]{0:T(1024)} %gq_ref.1, ...), custom_call_target="tpu_custom_call" | custom-call | flops 70000001024 | bytes 41943040 | tf_op jit(solution)/shard_map/main/pallas_call | solution.py:608
  107.5 16.2 %output.1 = bf16[12,64,2560]{2,1,0:T(8,128)(2,1)} custom-call(bf16[2,5,12,64,256]{4,3,2,1,0:T(8,128)(2,1)} %get-tuple-element.9.o_ref, bf16[320,2560]{1,0:T(8,128)(2,1)} %own_ref.1, bf16[2,4,320,2560]{3,2,1,0:T(8,128)(2,1)} %get-tuple-element.10.w_ref, bf16[12,64,2560]{2,1,0:T(8,128)(2,1)} %x_ref.1), custom_call_target="tpu_custom_call" | custom-call | flops 10066329600 | bytes 31457280 | tf_op jit(solution)/shard_map/output/pallas_call | solution.py:679
  123.7 10.4 %cache.1 = (bf16[12,1024,256]{2,1,0:T(8,128)(2,1)}, bf16[12,32,1024]{2,1,0:T(8,128)(2,1)}) custom-call(s32[12]{0:T(128)} %len_ref.3, bf16[12,4,2,64,256]{4,3,2,1,0:T(8,128)(2,1)} %bitcast.18, bf16[3,4,2,64,128]{4,3,2,1,0:T(8,128)(2,1)} %bitcast.20, bf16[12,1024,256]{2,1,0:T(8,128)(2,1)} %lat_ref.1, bf16[12,32,1024]{2,1,0:T(8,128)(2,1)} %bitcast.12), custom_call_target="tpu_custom_call" | custom-call | flops 4000000000 | bytes 20971520 | tf_op jit(solution)/shard_map/cache/pallas_call | solution.py:652

commit v5 on v4

--- a/solution.py
+++ b/solution.py
@@ -509,74 +509,74 @@
     pltpu.make_async_copy(o_own, o_out.at[0], load_sem.at[2]).wait()
 
 
-def cache_kernel(len_ref, c_ref, p_ref, lat_ref, pe_ref, lat_out, pe_out, fresh, fresh_pe):
+def finish_kernel(tiles, len_ref, o_ref, own_ref, w_ref, x_ref, c_ref, p_ref, lat_ref, pe_ref, y_ref, lat_out, pe_out, fresh):
     step = pl.program_id(0)
-    chip = lax.axis_index("tp") // 2
-    per, slots, _, toks, rank = c_ref.shape
-    rope = pe_ref.shape[1]
-    cache_len = lat_ref.shape[1]
+    me = lax.axis_index("tp")
+    odd, chip = lax.rem(me, 2), me // 2
+    _, quads, seqs, toks, depth = o_ref.shape
+    slots, w_rows, wide = w_ref.shape[1:]
+    rank = lat_ref.shape[2]
+    rope, cache_len = pe_ref.shape[1:]
     chunk = slots * 2 * toks
     words = rank // BLOCK
-    tile_row = lax.broadcasted_iota(jnp.int32, (16, BLOCK), 0)
+    length = len_ref[step]
 
     def slot_of(j):
         return lax.rem(chip - j + slots, slots)
 
-    def one_sequence(s, _):
-        length = len_ref[step * per + s]
+    def output():
+        y = x_ref[...].reshape(seqs * toks, wide).astype(F32)
+        for side in range(2):
+            w = w_ref[odd if side == 0 else 1 - odd].reshape(slots * w_rows, wide)
+            if side == 0:
+                w = jnp.concatenate([own_ref[...], w[w_rows:]], axis=0)
+            for quad in range(quads):
+                y = y + dot(o_ref[side, quad].reshape(seqs * toks, depth), w[quad * depth : (quad + 1) * depth])
+        y_ref[...] = y.astype(BF16).reshape(y_ref.shape)
+
+    def cache():
         for j in range(slots):
-            piece = c_ref[s, slot_of(j)].reshape(2 * toks, rank).astype(F32)
+            piece = c_ref[0, slot_of(j)].reshape(2 * toks, rank).astype(F32)
             for w in range(words):
                 fresh[w, BLOCK + j * 2 * toks : BLOCK + (j + 1) * 2 * toks] = piece[:, w * BLOCK : (w + 1) * BLOCK]
-        lat_out[s] = lat_ref[s]
+        lat_out[...] = lat_ref[...]
         base = (length // 16) * 16
         skew = length - base
-
-        def tile(k, partial):
-            at = pl.multiple_of(base + k * 16, 16)
+        tile_row = lax.broadcasted_iota(jnp.int32, (16, BLOCK), 0)
+        for k in range(chunk // 16 + 1):
+            at = pl.multiple_of(jnp.minimum(base + k * 16, cache_len - 16), 16)
             for w in range(words):
+                cols = slice(w * BLOCK, (w + 1) * BLOCK)
                 moved = fresh[w, pl.ds(BLOCK - skew + k * 16, 16), :].astype(BF16)
-                cols = slice(w * BLOCK, (w + 1) * BLOCK)
-                if partial:
-                    local = tile_row + k * 16 - skew
-                    moved = jnp.where((local >= 0) & (local < chunk), moved.astype(F32), lat_ref[s, pl.ds(at, 16), cols].astype(F32)).astype(BF16)
-                lat_out[s, pl.ds(at, 16), cols] = moved
-
-        for k in range(chunk // 16):
-            tile(k, k == 0)
-        pl.when(skew > 0)(functools.partial(tile, chunk // 16, True))
-        return 0
-
-    lax.fori_loop(0, per, one_sequence, 0)
-
-    for j in range(slots):
-        fresh_pe[cache_len - chunk + j * 2 * toks : cache_len - chunk + (j + 1) * 2 * toks] = p_ref[0, slot_of(j)].reshape(2 * toks, BLOCK).astype(F32)
-    old = pe_ref[...].reshape(per * rope, cache_len).astype(F32)
-    lane_seq = lax.broadcasted_iota(jnp.int32, (BLOCK, BLOCK), 1) // rope
-    row = lax.broadcasted_iota(jnp.int32, (BLOCK, BLOCK), 0)
-    for b in range(cache_len // BLOCK):
-        value = old[:, b * BLOCK : (b + 1) * BLOCK].T
-        for s in range(per):
-            length = len_ref[step * per + s]
-            moved = fresh_pe[pl.ds(b * BLOCK + cache_len - chunk - length, BLOCK), :]
-            local = row + (b * BLOCK - length)
-            value = jnp.where((lane_seq == s) & (local >= 0) & (local < chunk), moved, value)
-        pe_out[:, :, b * BLOCK : (b + 1) * BLOCK] = value.T.astype(BF16).reshape(per, rope, BLOCK)
-
-
-def output_kernel(o_ref, own_ref, w_ref, x_ref, y_ref):
-    odd = lax.rem(lax.axis_index("tp"), 2)
-    _, quads, seqs, toks, depth = o_ref.shape
-    slots, rows, wide = w_ref.shape[1:]
-    y = x_ref[...].reshape(seqs * toks, wide).astype(F32)
-    for side in range(2):
-        parity = odd if side == 0 else 1 - odd
-        w = w_ref[parity].reshape(slots * rows, wide)
-        if side == 0:
-            w = jnp.concatenate([own_ref[...], w[rows:]], axis=0)
-        for quad in range(quads):
-            y = y + dot(o_ref[side, quad].reshape(seqs * toks, depth), w[quad * depth : (quad + 1) * depth])
-    y_ref[...] = y.astype(BF16).reshape(y_ref.shape)
+                if k == 0 or k == chunk // 16:
+                    local = tile_row + (at - length)
+                    shown = (local >= 0) & (local < chunk) if k == 0 else (local < chunk)
+                    if k == 0:
+                        rest = lat_ref[0, pl.ds(at, 16), cols]
+                    else:
+                        shown = shown & (skew > 0)
+                        rest = lat_out[0, pl.ds(at, 16), cols]
+                    moved = jnp.where(shown, moved.astype(F32), rest.astype(F32)).astype(BF16)
+                lat_out[0, pl.ds(at, 16), cols] = moved
+
+        turned = jnp.concatenate([p_ref[0, slot_of(j)].reshape(2 * toks, BLOCK).astype(F32).T for j in range(slots)], axis=1)
+        group = lax.rem(step, BLOCK // rope)
+        mine = turned[:rope]
+        for g in range(1, BLOCK // rope):
+            mine = jnp.where(group == g, turned[g * rope : (g + 1) * rope], mine)
+        mine = jnp.concatenate([mine, jnp.zeros((rope, cache_len - chunk), F32)], axis=1)
+        mine = pltpu.roll(mine, length, axis=1)
+        spot = lax.broadcasted_iota(jnp.int32, (rope, cache_len), 1) - length
+        pe_out[0] = jnp.where((spot >= 0) & (spot < chunk), mine, pe_ref[0].astype(F32)).astype(BF16)
+
+    @pl.when(step < tiles)
+    def _():
+        output()
+        cache()
+
+    @pl.when(step >= tiles)
+    def _():
+        cache()
 
 
 def solution(mesh):
@@ -647,50 +647,50 @@
             name="main",
         )(lengths, hidden, norm_in, w_dq, norm_q, wdkv_t, norm_kv, cos_t, sin_t, wq_t, wk_t, wv_t, w_out, cache_lat, pe_t)
 
-        c_all = c_all.reshape(seqs, slots, 2, toks, rank)
-        p_all = p_all.reshape(groups, slots, 2, toks, BLOCK)
-        lat_new, pe_new = pl.pallas_call(
-            cache_kernel,
+        part = wide
+        tiles = dim // part
+        tile = lambda i: jnp.minimum(i, tiles - 1)
+        y, lat_new, pe_new = pl.pallas_call(
+            functools.partial(finish_kernel, tiles),
             grid_spec=pltpu.PrefetchScalarGridSpec(
                 num_scalar_prefetch=1,
-                grid=(groups,),
+                grid=(seqs,),
                 in_specs=[
-                    pl.BlockSpec((per, slots, 2, toks, rank), lambda i, n: (i, 0, 0, 0, 0)),
-                    pl.BlockSpec((1, slots, 2, toks, BLOCK), lambda i, n: (i, 0, 0, 0, 0)),
-                    pl.BlockSpec((per, cache_len, rank), lambda i, n: (i, 0, 0)),
-                    pl.BlockSpec((per, rope, cache_len), lambda i, n: (i, 0, 0)),
+                    pl.BlockSpec(o_all.shape, lambda i, n: (0, 0, 0, 0, 0), pipeline_mode=pl.Buffered(1)),
+                    pl.BlockSpec((w_out.shape[0], part), lambda i, n: (0, tile(i))),
+                    pl.BlockSpec(wo_all.shape[:3] + (part,), lambda i, n: (0, 0, 0, tile(i))),
+                    pl.BlockSpec((seqs, toks, part), lambda i, n: (0, 0, tile(i))),
+                    pl.BlockSpec((1, slots, 2, toks, rank), lambda i, n: (i, 0, 0, 0, 0)),
+                    pl.BlockSpec((1, slots, 2, toks, BLOCK), lambda i, n: (i // per, 0, 0, 0, 0)),
+                    pl.BlockSpec((1, cache_len, rank), lambda i, n: (i, 0, 0)),
+                    pl.BlockSpec((1, rope, cache_len), lambda i, n: (i, 0, 0)),
                 ],
                 out_specs=[
-                    pl.BlockSpec((per, cache_len, rank), lambda i, n: (i, 0, 0)),
-                    pl.BlockSpec((per, rope, cache_len), lambda i, n: (i, 0, 0)),
+                    pl.BlockSpec((seqs, toks, part), lambda i, n: (0, 0, tile(i))),
+                    pl.BlockSpec((1, cache_len, rank), lambda i, n: (i, 0, 0)),
+                    pl.BlockSpec((1, rope, cache_len), lambda i, n: (i, 0, 0)),
                 ],
-                scratch_shapes=[
-                    pltpu.VMEM((rank // BLOCK, chunk + 2 * BLOCK, BLOCK), F32),
-                    pltpu.VMEM((2 * cache_len - chunk, BLOCK), F32),
-                ],
+                scratch_shapes=[pltpu.VMEM((rank // BLOCK, chunk + 2 * BLOCK, BLOCK), F32)],
             ),
-            out_shape=[jax.ShapeDtypeStruct(cache_lat.shape, BF16), jax.ShapeDtypeStruct(pe_t.shape, BF16)],
+            out_shape=[
+                jax.ShapeDtypeStruct(hidden.shape, BF16),
+                jax.ShapeDtypeStruct(cache_lat.shape, BF16),
+                jax.ShapeDtypeStruct(pe_t.shape, BF16),
+            ],
             compiler_params=pltpu.CompilerParams(vmem_limit_bytes=63 * MIB),
-            cost_estimate=pl.CostEstimate(flops=4 * 10**9, bytes_accessed=20 * MIB, transcendentals=0),
-            name="cache",
-        )(lengths, c_all, p_all, cache_lat, pe_t)
-
-        part = 512
-        y = pl.pallas_call(
-            output_kernel,
-            grid=(dim // part,),
-            in_specs=[
-                pl.BlockSpec(o_all.shape, lambda i: (0, 0, 0, 0, 0), pipeline_mode=pl.Buffered(1)),
-                pl.BlockSpec((w_out.shape[0], part), lambda i: (0, i)),
-                pl.BlockSpec(wo_all.shape[:3] + (part,), lambda i: (0, 0, 0, i)),
-                pl.BlockSpec((seqs, toks, part), lambda i: (0, 0, i)),
-            ],
-            out_specs=pl.BlockSpec((seqs, toks, part), lambda i: (0, 0, i)),
-            out_shape=jax.ShapeDtypeStruct(hidden.shape, BF16),
-            compiler_params=pltpu.CompilerParams(vmem_limit_bytes=63 * MIB),
-            cost_estimate=pl.CostEstimate(flops=2 * seqs * toks * dim * dim, bytes_accessed=30 * MIB, transcendentals=0),
-            name="output",
-        )(o_all, w_out, wo_all, hidden)
+            cost_estimate=pl.CostEstimate(flops=2 * seqs * toks * dim * dim, bytes_accessed=50 * MIB, transcendentals=0),
+            name="finish",
+        )(
+            lengths,
+            o_all,
+            w_out,
+            wo_all,
+            hidden,
+            c_all.reshape(seqs, slots, 2, toks, rank),
+            p_all.reshape(groups, slots, 2, toks, BLOCK),
+            cache_lat,
+            pe_t,
+        )
         return y, lat_new, pe_new.transpose(0, 2, 1)
 
     spec_tok = P("dp", "tp", None)

time: 134 us -> 132 us (0.985)
  Pallas kernels: 134 us -> 130 us
    pallas_call x2 -> x1, Pallas kernels: 26.6 us -> 23.5 us  [local_step(): pl.pallas_call(functools.partial(finish_kernel, tiles), grid_spec=pltpu.P...]
where the time goes in v5:
time: 132 us; the launch traced here: 131 us
  Pallas kernels  130 us (98%)
    pallas_call x1, Pallas kernels, local_step(): pl.pallas_call(functools.partial(main_kernel, (size, paired)), in_specs=[...  107 us
    pallas_call x1, Pallas kernels, local_step(): pl.pallas_call(functools.partial(finish_kernel, tiles), grid_spec=pltpu.P...  23.5 us

profile of v5, /device:TPU:81, one launch (start us, length us, event | category | flops | bytes accessed | tf_op | source)
XLA Modules:
  0.0 131.2 jit_solution(7419888919590191325)
XLA Ops:
  0.6 106.9 %main.1 = (bf16[12,512,256]{2,1,0:T(8,128)(2,1)}, bf16[3,512,128]{2,1,0:T(8,128)(2,1)}, bf16[2,5,12,64,256]{4,3,2,1,0:T(8,128)(2,1)}, bf16[2,4,320,2560]{3,2,1,0:T(8,128)(2,1)}) custom-call(s32[12]{0:T(128)} %len_ref.3, bf16[12,64,2560]{2,1,0:T(8,128)(2,1)} %x_ref.1, f32[2560]{0:T(1024)} %g1_ref.1, bf16[2560,768]{1,0:T(8,128)(2,1)} %wdq_hbm.1, f32[768]{0:T(1024)} %gq_ref.1, ...), custom_call_target="tpu_custom_call" | custom-call | flops 70000001024 | bytes 41943040 | tf_op jit(solution)/shard_map/main/pallas_call | solution.py:608
  107.5 23.5 %finish.1 = (bf16[12,64,2560]{2,1,0:T(8,128)(2,1)}, bf16[12,1024,256]{2,1,0:T(8,128)(2,1)}, bf16[12,32,1024]{2,1,0:T(8,128)(2,1)}) custom-call(s32[12]{0:T(128)} %len_ref.3, bf16[2,5,12,64,256]{4,3,2,1,0:T(8,128)(2,1)} %get-tuple-element.10.o_ref, bf16[320,2560]{1,0:T(8,128)(2,1)} %own_ref.1, bf16[2,4,320,2560]{3,2,1,0:T(8,128)(2,1)} %get-tuple-element.11.w_ref, ...), custom_call_target="tpu_custom_call" | custom-call | flops 10066329600 | bytes 52428800 | tf_op jit(solution)/shard_map/finish/pallas_call | solution.py:653
